TPU v7x, 32 devices: a whole 2x2x4 slice. The times are simulated.
32 devices in a mesh: pb: 4 (over y, x), neg: 8 (over z, core).
Axes of the slice: x: 2, y: 2, z: 4, core: 2. Of those that a mesh axis runs over, the one named last changes fastest.
Arguments:
- hidden: bfloat16 [4, 32, 128, 1024], P('pb', 'neg'), may hold values from -6 to 6
- lengths: int32 [4, 32], P('pb', 'neg'), may hold values from 32 to 128
- teacher: float32 [4, 32], P('pb', 'neg'), may hold values from -8 to 8
- norm_gain: float32 [1024], replicated, may hold values from 0.1 to 1.9
- final_gain: float32 [1024], replicated, may hold values from 0.1 to 1.9
- score_vector: float32 [1024], replicated, may hold values from -0.1875 to 0.1875
- query_weight: bfloat16 [1024, 1024], P(('pb', 'neg')), may hold values from -0.1875 to 0.1875
- key_matrix: bfloat16 [1024, 512], P(('pb', 'neg')), may hold values from -0.1875 to 0.1875
- value_matrix: bfloat16 [1024, 512], P(('pb', 'neg')), may hold values from -0.1875 to 0.1875
- out_weight: bfloat16 [1024, 1024], P(None, ('pb', 'neg')), may hold values from -0.1875 to 0.1875
Outputs:
- scores: float32 [4, 32], P('pb', 'neg')
- loss: float32 [], replicated
- grad_hidden: bfloat16 [4, 32, 128, 1024], P('pb', 'neg')
- grad_query: float32 [1024, 1024], P(('pb', 'neg'))
- grad_key: float32 [1024, 512], P(('pb', 'neg'))
- grad_value: float32 [1024, 512], P(('pb', 'neg'))
- grad_out: float32 [1024, 1024], P(None, ('pb', 'neg'))
Inputs may be any that keep to these rules, and one draw needn't show every extreme that they name: `lengths`: the number of real tokens of the pair; its other positions out of 128 are padding.
All inputs are finite; a program needn't handle non-finite values.
Results may differ from a plain program's by a relative error of at most 0.013.
Values may be sent and summed in bfloat16 or wider, within the bound.
A program may use at most 64 MiB of HBM per device.

v0:
```python
import functools

import jax
import jax.numpy as jnp
from jax import lax
from jax.experimental import pallas as pl
from jax.experimental.pallas import tpu as pltpu
from jax.sharding import PartitionSpec as P

HEAD_WIDTH = 128
MESH_ID = pl.DeviceIdType.MESH

EPSILON = 1e-06
ROPE_BASE = 1000000.0
TEACHER_TEMP = 2.0
GRAD_SCALE = 512.0


def rope_tables(seq_len, head_size):
    half = head_size // 2
    freqs = ROPE_BASE ** (-(jnp.arange(half, dtype=jnp.float32) * 2.0) / head_size)
    angles = jnp.arange(seq_len, dtype=jnp.float32)[:, None] * freqs[None, :]
    angles = jnp.concatenate([angles, angles], axis=1)
    return (jnp.cos(angles), jnp.sin(angles))


def rotate_half(vector):
    half = vector.shape[-1] // 2
    return jnp.concatenate([-vector[..., half:], vector[..., :half]], axis=-1)


def unrotate_half(vector):
    half = vector.shape[-1] // 2
    return jnp.concatenate([vector[..., half:], -vector[..., :half]], axis=-1)


def forward_pairs(
    tokens_in,
    lengths_here,
    norm_gain,
    final_gain,
    score_vector,
    query_weight,
    key_matrix,
    value_matrix,
    out_weight,
):
    pair_count, seq_len, model_width = tokens_in.shape
    head_count = query_weight.shape[1] // HEAD_WIDTH
    group_count = key_matrix.shape[1] // HEAD_WIDTH
    group_size = head_count // group_count
    inputs_wide = tokens_in.astype(jnp.float32)
    inv_rms = lax.rsqrt(jnp.mean(inputs_wide * inputs_wide, axis=-1, keepdims=True) + EPSILON)
    normed = (inputs_wide * inv_rms * norm_gain).astype(jnp.bfloat16)
    flat_rows = normed.reshape(pair_count * seq_len, model_width)
    key_proj = jnp.dot(flat_rows, key_matrix, preferred_element_type=jnp.float32).reshape(
        pair_count, seq_len, group_count, HEAD_WIDTH
    )
    value_proj = jnp.dot(flat_rows, value_matrix, preferred_element_type=jnp.float32).reshape(
        pair_count, seq_len, group_count, HEAD_WIDTH
    )
    positions = jnp.arange(seq_len, dtype=jnp.int32)
    last_index = lengths_here - 1
    onehot = (positions[None, :] == last_index[:, None]).astype(jnp.float32)
    normed_last = jnp.take_along_axis(normed, last_index[:, None, None], axis=1)[:, 0]
    query_proj = jnp.dot(normed_last, query_weight, preferred_element_type=jnp.float32).reshape(
        pair_count, head_count, HEAD_WIDTH
    )
    query_scale = lax.rsqrt(jnp.mean(query_proj * query_proj, axis=-1, keepdims=True) + EPSILON)
    query_unit = query_proj * query_scale
    key_scale = lax.rsqrt(jnp.mean(key_proj * key_proj, axis=-1, keepdims=True) + EPSILON)
    key_unit = key_proj * key_scale
    cos_table, sin_table = rope_tables(seq_len, HEAD_WIDTH)
    cos_query = jnp.dot(onehot, cos_table, precision=lax.Precision.HIGHEST)
    sin_query = jnp.dot(onehot, sin_table, precision=lax.Precision.HIGHEST)
    query_rot = (
        query_unit * cos_query[:, None, :] + rotate_half(query_unit) * sin_query[:, None, :]
    ).astype(jnp.bfloat16)
    key_rot = (
        key_unit * cos_table[None, :, None, :] + rotate_half(key_unit) * sin_table[None, :, None, :]
    ).astype(jnp.bfloat16)
    value_cast = value_proj.astype(jnp.bfloat16)
    grouped = query_rot.reshape(pair_count, group_count, group_size, HEAD_WIDTH)
    logits = jnp.einsum(
        "pkgd,pskd->pkgs", grouped, key_rot, preferred_element_type=jnp.float32
    ) * HEAD_WIDTH ** (-0.5)
    visible = (positions[None, :] <= last_index[:, None])[:, None, None, :]
    expos = jnp.where(visible, jnp.exp(logits), 0.0)
    attention_weights = expos / jnp.sum(expos, axis=-1, keepdims=True)
    probs_cast = attention_weights.astype(jnp.bfloat16)
    context = jnp.einsum(
        "pkgs,pskd->pkgd", probs_cast, value_cast, preferred_element_type=jnp.float32
    )
    context = context.astype(jnp.bfloat16).reshape(pair_count, head_count * HEAD_WIDTH)
    attended = jnp.dot(context, out_weight, preferred_element_type=jnp.float32)
    residual = jnp.take_along_axis(inputs_wide, last_index[:, None, None], axis=1)[:, 0] + attended
    out_scale = lax.rsqrt(jnp.mean(residual * residual, axis=-1, keepdims=True) + EPSILON)
    out_unit = residual * out_scale
    scores_here = jnp.sum(out_unit * final_gain * score_vector, axis=-1)
    stored = (
        tokens_in,
        onehot,
        inv_rms,
        normed,
        normed_last,
        query_unit,
        query_scale,
        key_unit,
        key_scale,
        cos_query,
        sin_query,
        cos_table,
        sin_table,
        query_rot,
        key_rot,
        value_cast,
        attention_weights,
        probs_cast,
        context,
        out_unit,
        out_scale,
    )
    return (scores_here, stored)


def backward_pairs(
    stored,
    grad_score,
    norm_gain,
    final_gain,
    score_vector,
    query_weight,
    key_matrix,
    value_matrix,
    out_weight,
):
    (
        tokens_in,
        onehot,
        inv_rms,
        normed,
        normed_last,
        query_unit,
        query_scale,
        key_unit,
        key_scale,
        cos_query,
        sin_query,
        cos_table,
        sin_table,
        query_rot,
        key_rot,
        value_cast,
        attention_weights,
        probs_cast,
        context,
        out_unit,
        out_scale,
    ) = stored
    pair_count, seq_len, model_width = tokens_in.shape
    head_count = query_weight.shape[1] // HEAD_WIDTH
    group_count = key_matrix.shape[1] // HEAD_WIDTH
    group_size = head_count // group_count
    grad_unit = grad_score[:, None] * score_vector * final_gain
    grad_resid = out_scale * (
        grad_unit - out_unit * jnp.mean(grad_unit * out_unit, axis=-1, keepdims=True)
    )
    grad_resid_cast = grad_resid.astype(jnp.bfloat16)
    grad_context = jnp.dot(
        grad_resid_cast, out_weight.T, preferred_element_type=jnp.float32
    ).astype(jnp.bfloat16)
    grad_context = grad_context.reshape(pair_count, group_count, group_size, HEAD_WIDTH)
    grad_probs = jnp.einsum(
        "pkgd,pskd->pkgs", grad_context, value_cast, preferred_element_type=jnp.float32
    )
    grad_vals = jnp.einsum(
        "pkgs,pkgd->pskd", probs_cast, grad_context, preferred_element_type=jnp.float32
    )
    spread = jnp.sum(attention_weights * grad_probs, axis=-1, keepdims=True)
    logit_gradient = (attention_weights * (grad_probs - spread)).astype(jnp.bfloat16)
    grouped = query_rot.reshape(pair_count, group_count, group_size, HEAD_WIDTH)
    rotated_query_gradient = jnp.einsum(
        "pkgs,pskd->pkgd", logit_gradient, key_rot, preferred_element_type=jnp.float32
    ) * HEAD_WIDTH ** (-0.5)
    rotated_query_gradient = rotated_query_gradient.reshape(pair_count, head_count, HEAD_WIDTH)
    grad_krot = jnp.einsum(
        "pkgs,pkgd->pskd", logit_gradient, grouped, preferred_element_type=jnp.float32
    ) * HEAD_WIDTH ** (-0.5)
    grad_qunit = rotated_query_gradient * cos_query[:, None, :] + unrotate_half(
        rotated_query_gradient * sin_query[:, None, :]
    )
    grad_kunit = grad_krot * cos_table[None, :, None, :] + unrotate_half(
        grad_krot * sin_table[None, :, None, :]
    )
    grad_qproj = query_scale * (
        grad_qunit - query_unit * jnp.mean(grad_qunit * query_unit, axis=-1, keepdims=True)
    )
    grad_kproj = key_scale * (
        grad_kunit - key_unit * jnp.mean(grad_kunit * key_unit, axis=-1, keepdims=True)
    )
    grad_q_cast = grad_qproj.reshape(pair_count, head_count * HEAD_WIDTH).astype(jnp.bfloat16)
    grad_k_cast = grad_kproj.reshape(pair_count * seq_len, group_count * HEAD_WIDTH).astype(
        jnp.bfloat16
    )
    grad_v_cast = grad_vals.reshape(pair_count * seq_len, group_count * HEAD_WIDTH).astype(
        jnp.bfloat16
    )
    flat_rows = normed.reshape(pair_count * seq_len, model_width)
    last_rows = jnp.concatenate([normed_last, grad_resid_cast, grad_q_cast, context], axis=1)
    grad_kv = jnp.dot(
        flat_rows.T,
        jnp.concatenate([grad_k_cast, grad_v_cast], axis=1),
        preferred_element_type=jnp.float32,
    )
    grad_normed = jnp.dot(grad_k_cast, key_matrix.T, preferred_element_type=jnp.float32)
    grad_normed = grad_normed + jnp.dot(
        grad_v_cast, value_matrix.T, preferred_element_type=jnp.float32
    )
    grad_normed = grad_normed.reshape(pair_count, seq_len, model_width)
    grad_last = jnp.dot(grad_q_cast, query_weight.T, preferred_element_type=jnp.float32)
    grad_normed = grad_normed + onehot[:, :, None] * grad_last[:, None, :]
    inputs_wide = tokens_in.astype(jnp.float32)
    grad_scaled = grad_normed * norm_gain
    grad_input = inv_rms * grad_scaled - inputs_wide * inv_rms * inv_rms * inv_rms * jnp.mean(
        grad_scaled * inputs_wide, axis=-1, keepdims=True
    )
    grad_input = grad_input + onehot[:, :, None] * grad_resid[:, None, :]
    return (grad_input.astype(jnp.bfloat16), last_rows, grad_kv)


class Place:
    def __init__(self):
        self.pb_count = lax.axis_size("pb")
        self.neg_count = lax.axis_size("neg")
        self.line_count = self.neg_count // 2
        self.pb = lax.axis_index("pb")
        neg = lax.axis_index("neg")
        self.line = neg // 2
        self.core = neg % 2
        self.partner = 1 - self.core

    def slot(self, pb, line, core):
        return pb * self.neg_count + line * 2 + core

    def line_peer(self, step):
        return lax.rem(self.line + step, self.line_count)

    def pb_peer(self, step):
        return lax.rem(self.pb + step, self.pb_count)

    def to_line(self, line):
        return (self.pb, line * 2 + self.core)

    def to_pb(self, pb):
        return (pb, self.line * 2 + self.core)

    def to_partner(self):
        return (self.pb, self.line * 2 + self.partner)

    def greet(self):
        barrier = pltpu.get_barrier_semaphore()
        targets = [self.to_line(self.line_peer(k)) for k in range(1, self.line_count)]
        targets += [self.to_pb(self.pb_peer(k)) for k in range(1, self.pb_count)]
        targets += [self.to_partner()]
        for target in targets:
            pl.semaphore_signal(barrier, inc=1, device_id=target, device_id_type=MESH_ID)
        pl.semaphore_wait(barrier, len(targets))


def remote(src, dst, send_sem, recv_sem, target):
    return pltpu.make_async_remote_copy(
        src_ref=src,
        dst_ref=dst,
        send_sem=send_sem,
        recv_sem=recv_sem,
        device_id=target,
        device_id_type=MESH_ID,
    )


def gather_sems(pb_count, neg_count):
    line_count = neg_count // 2
    return [
        pltpu.SemaphoreType.DMA((line_count,)),
        pltpu.SemaphoreType.DMA((line_count,)),
        pltpu.SemaphoreType.DMA((2, line_count)),
        pltpu.SemaphoreType.DMA((2, line_count)),
        pltpu.SemaphoreType.DMA((2, line_count)),
        pltpu.SemaphoreType.DMA((2, line_count)),
        pltpu.SemaphoreType.DMA((pb_count, line_count)),
        pltpu.SemaphoreType.DMA((pb_count, line_count)),
        pltpu.SemaphoreType.DMA,
    ]


class Gather:
    def __init__(self, place, own, full, sems):
        self.place, self.own, self.full = place, own, full
        self.line_send, self.line_recv, self.pb_send, self.pb_recv = sems[:4]
        self.half_send, self.half_recv = sems[4:6]
        self.core_send, self.core_recv, self.local_sem = sems[6:]
        self.sent = []
        across = place.pb + 1 - 2 * (place.pb % 2)
        along = place.pb + 2 - 4 * (place.pb // 2)
        self.near = (across, along)
        self.corner = 3 - place.pb

    def rows(self, pb, line, core):
        size = self.own.shape[0]
        start = self.place.slot(pb, line, core) * size
        return self.full.at[pl.ds(pl.multiple_of(start, size), size)]

    def send(self, src, dst, send_sem, recv_sem, target):
        copy = remote(src, dst, send_sem, recv_sem, target)
        copy.start()
        self.sent.append(copy)

    def spread(self, src, line):
        at = self.place
        dst = self.rows(at.pb, line, at.core)
        for side in range(2):
            self.send(
                src, dst, self.pb_send.at[side, line], self.pb_recv.at[side, line], at.to_pb(self.near[side])
            )
        self.pass_on(src, at.pb, line)

    def pass_on(self, src, pb, line):
        at = self.place
        dst = self.rows(pb, line, at.core)
        self.send(src, dst, self.core_send.at[pb, line], self.core_recv.at[pb, line], at.to_partner())

    def arrive(self, block, recv_sem):
        remote(block, block, self.local_sem, recv_sem, self.place.to_partner()).wait_recv()

    def start(self):
        at = self.place
        mine = self.rows(at.pb, at.line, at.core)
        self.local = pltpu.make_async_copy(self.own, mine, self.local_sem)
        self.local.start()
        for k in range(1, at.line_count):
            line = at.line_peer(k)
            self.send(
                self.own, mine, self.line_send.at[k], self.line_recv.at[at.line], at.to_line(line)
            )
        self.spread(self.own, at.line)

    def middle(self):
        at = self.place
        for k in range(1, at.line_count):
            line = at.line_peer(k)
            block = self.rows(at.pb, line, at.core)
            self.arrive(block, self.line_recv.at[line])
            self.spread(block, line)

    def half(self, block, side):
        width = block.shape[1] // 2
        return block.at[:, pl.ds(side * width, width)]

    def relay(self):
        at = self.place
        for step in range(at.line_count):
            line = at.line_peer(step)
            for side in range(2):
                block = self.rows(self.near[side], line, at.core)
                self.arrive(block, self.pb_recv.at[side, line])
                part = self.half(block, side)
                self.send(
                    part,
                    part,
                    self.half_send.at[side, line],
                    self.half_recv.at[side, line],
                    at.to_pb(self.near[1 - side]),
                )
                self.pass_on(block, self.near[side], line)

    def finish(self):
        at = self.place
        for step in range(at.line_count):
            line = at.line_peer(step)
            block = self.rows(self.corner, line, at.core)
            for side in range(2):
                self.arrive(self.half(block, side), self.half_recv.at[side, line])
            self.pass_on(block, self.corner, line)
        for pb in range(at.pb_count):
            for line in range(at.line_count):
                self.arrive(self.rows(pb, line, at.partner), self.core_recv.at[pb, line])
        for copy in self.sent:
            copy.wait_send()
        self.local.wait()


def gather_kernel(count, *refs):
    place = Place()
    place.greet()
    owns, fulls, sems = refs[:count], refs[count : 2 * count], refs[2 * count :]
    each = len(sems) // count
    gathers = [
        Gather(place, owns[i], fulls[i], sems[i * each : (i + 1) * each]) for i in range(count)
    ]
    for gather in gathers:
        gather.start()
    for gather in gathers:
        gather.middle()
    for gather in gathers:
        gather.relay()
    for gather in gathers:
        gather.finish()


VMEM_SPEC = pl.BlockSpec(memory_space=pltpu.VMEM)


def gather_weights(shares, pb_count, neg_count):
    count = len(shares)
    return pl.pallas_call(
        functools.partial(gather_kernel, count),
        out_shape=tuple(
            jax.ShapeDtypeStruct((w.shape[0] * pb_count * neg_count, w.shape[1]), w.dtype)
            for w in shares
        ),
        in_specs=[VMEM_SPEC] * count,
        out_specs=(VMEM_SPEC,) * count,
        scratch_shapes=gather_sems(pb_count, neg_count) * count,
        compiler_params=pltpu.CompilerParams(
            collective_id=0, has_side_effects=True, vmem_limit_bytes=32 * 2**20
        ),
    )(*shares)


def listing_kernel(own, full, send, recv, local_sem):
    at = Place()
    barrier = pltpu.get_barrier_semaphore()
    neg = lax.axis_index("neg")
    peers = [lax.rem(neg + k, at.neg_count) for k in range(1, at.neg_count)]
    for peer in peers:
        pl.semaphore_signal(barrier, inc=1, device_id=(at.pb, peer), device_id_type=MESH_ID)
    pl.semaphore_wait(barrier, len(peers))
    copies = []
    local = pltpu.make_async_copy(own, full.at[neg], local_sem)
    local.start()
    for k, peer in enumerate(peers):
        copy = remote(own, full.at[neg], send.at[k], recv.at[neg], (at.pb, peer))
        copy.start()
        copies.append(copy)
    local.wait()
    for peer in peers:
        block = full.at[peer]
        remote(block, block, local_sem, recv.at[peer], (at.pb, peer)).wait_recv()
    for copy in copies:
        copy.wait_send()


def exchange_listing(own, neg_count):
    return pl.pallas_call(
        listing_kernel,
        out_shape=jax.ShapeDtypeStruct((neg_count,) + own.shape, own.dtype),
        in_specs=[VMEM_SPEC],
        out_specs=VMEM_SPEC,
        scratch_shapes=[
            pltpu.SemaphoreType.DMA((neg_count,)),
            pltpu.SemaphoreType.DMA((neg_count,)),
            pltpu.SemaphoreType.DMA,
        ],
        compiler_params=pltpu.CompilerParams(collective_id=1, has_side_effects=True),
    )(own)


def reduce_kernel(
    partial,
    last_rows,
    loss_row,
    reduced,
    all_rows,
    all_losses,
    from_core,
    paired,
    from_pb,
    summed,
    from_line,
    core_send,
    core_recv,
    pb_send,
    pb_recv,
    line_send,
    line_recv,
    loss_send,
    loss_recv,
    loss_local,
    *sems,
):
    at = Place()
    at.greet()
    gather = Gather(at, last_rows, all_rows, sems)
    copies = []

    def send(src, dst, send_sem, recv_sem, target):
        copy = remote(src, dst, send_sem, recv_sem, target)
        copy.start()
        copies.append(copy)

    def arrive(block, recv_sem):
        remote(block, block, loss_local, recv_sem, at.to_partner()).wait_recv()

    for k in range(1, at.pb_count + 1):
        pb = at.pb_peer(k % at.pb_count)
        send(
            partial.at[pb, :, at.partner],
            from_core.at[pb],
            core_send.at[pb],
            core_recv.at[pb],
            at.to_partner(),
        )
    gather.start()
    local = pltpu.make_async_copy(loss_row, all_losses.at[at.pb], loss_local)
    local.start()
    for k in range(1, at.pb_count):
        send(
            loss_row, all_losses.at[at.pb], loss_send.at[k], loss_recv.at[at.pb], at.to_pb(at.pb_peer(k))
        )
    for k in range(1, at.pb_count + 1):
        pb = at.pb_peer(k % at.pb_count)
        arrive(from_core.at[pb], core_recv.at[pb])
        both = partial[pb, :, at.core].astype(jnp.float32) + from_core[pb].astype(jnp.float32)
        paired[pb] = both.astype(jnp.bfloat16)
        if k < at.pb_count:
            send(
                paired.at[pb], from_pb.at[at.pb], pb_send.at[k], pb_recv.at[at.pb], at.to_pb(pb)
            )
    gather.middle()
    gather.relay()
    for k in range(1, at.pb_count):
        pb = at.pb_peer(k)
        arrive(from_pb.at[pb], pb_recv.at[pb])
    for step in range(1, at.line_count + 1):
        line = at.line_peer(step % at.line_count)
        total = paired[at.pb, line].astype(jnp.float32)
        for k in range(1, at.pb_count):
            total = total + from_pb[at.pb_peer(k), line].astype(jnp.float32)
        if step < at.line_count:
            summed[line] = total.astype(jnp.bfloat16)
            send(
                summed.at[line],
                from_line.at[at.line],
                line_send.at[line],
                line_recv.at[at.line],
                at.to_line(line),
            )
    for step in range(1, at.line_count):
        line = at.line_peer(step)
        arrive(from_line.at[line], line_recv.at[line])
        total = total + from_line[line].astype(jnp.float32)
    reduced[...] = total
    gather.finish()
    local.wait()
    for k in range(1, at.pb_count):
        pb = at.pb_peer(k)
        arrive(all_losses.at[pb], loss_recv.at[pb])
    for copy in copies:
        copy.wait_send()


def reduce_gradients(grad_kv, last_rows, loss_row, pb_count, neg_count):
    line_count = neg_count // 2
    share = grad_kv.shape[0] // (pb_count * neg_count)
    width = grad_kv.shape[1]
    partial = grad_kv.reshape(pb_count, line_count, 2, share, width)
    block = (pb_count, line_count, share, width)
    dma = pltpu.SemaphoreType.DMA
    return pl.pallas_call(
        reduce_kernel,
        out_shape=(
            jax.ShapeDtypeStruct((share, width), jnp.float32),
            jax.ShapeDtypeStruct((last_rows.shape[0] * pb_count * neg_count, last_rows.shape[1]), last_rows.dtype),
            jax.ShapeDtypeStruct((pb_count,) + loss_row.shape, loss_row.dtype),
        ),
        in_specs=[VMEM_SPEC] * 3,
        out_specs=(VMEM_SPEC,) * 3,
        scratch_shapes=[
            pltpu.VMEM(block, jnp.bfloat16),
            pltpu.VMEM(block, jnp.bfloat16),
            pltpu.VMEM(block, jnp.bfloat16),
            pltpu.VMEM(block[1:], jnp.bfloat16),
            pltpu.VMEM(block[1:], jnp.bfloat16),
            dma((pb_count,)),
            dma((pb_count,)),
            dma((pb_count,)),
            dma((pb_count,)),
            dma((line_count,)),
            dma((line_count,)),
            dma((pb_count,)),
            dma((pb_count,)),
            dma,
        ]
        + gather_sems(pb_count, neg_count),
        compiler_params=pltpu.CompilerParams(
            collective_id=2, has_side_effects=True, vmem_limit_bytes=40 * 2**20
        ),
    )(partial, last_rows, loss_row)


def shards(
    hidden,
    lengths,
    teacher,
    norm_gain,
    final_gain,
    score_vector,
    query_weight,
    key_matrix,
    value_matrix,
    out_weight,
):
    both = ("pb", "neg")
    width = query_weight.shape[1]
    kv_width = key_matrix.shape[1]
    shares = (query_weight, key_matrix, value_matrix, out_weight.T)
    pb_count, neg_count = lax.axis_size("pb"), lax.axis_size("neg")
    even = all(w.shape[0] % 16 == 0 and w.shape[1] % (2 * HEAD_WIDTH) == 0 for w in shares)
    own_kernels = even and pb_count == 4 and neg_count % 2 == 0
    if own_kernels:
        full_query, full_key, full_value, full_out_t = gather_weights(shares, pb_count, neg_count)
    else:
        packed = jnp.concatenate(shares, axis=1)
        everything = lax.all_gather(packed, both, axis=0, tiled=True)
        full_query = everything[:, :width]
        full_key = everything[:, width : width + kv_width]
        full_value = everything[:, width + kv_width : width + 2 * kv_width]
        full_out_t = everything[:, width + 2 * kv_width :]
    scores_here, stored = forward_pairs(
        hidden[0],
        lengths[0],
        norm_gain,
        final_gain,
        score_vector,
        full_query,
        full_key,
        full_value,
        full_out_t.T,
    )
    pair_count = scores_here.shape[0]
    row = lax.axis_index("pb")
    listing = jnp.concatenate([scores_here, teacher[0]])[None]
    if own_kernels:
        lanes = jnp.pad(listing, ((0, 0), (0, HEAD_WIDTH - 2 * pair_count)))
        listed = exchange_listing(lanes, neg_count)[:, 0, : 2 * pair_count]
    else:
        listed = lax.all_gather(listing, "neg", axis=0, tiled=True)
    all_scores = listed[:, :pair_count]
    all_scaled = listed[:, pair_count:] / TEACHER_TEMP
    my_total_s = jnp.sum(jnp.exp(all_scores))
    expo_t = jnp.exp(all_scaled)
    my_total_t = jnp.sum(expo_t)
    loss_here = jnp.sum(
        expo_t
        / my_total_t
        * (all_scaled - jnp.log(my_total_t) - (all_scores - jnp.log(my_total_s)))
    )
    prob_s = jnp.exp(scores_here) / my_total_s
    prob_t = jnp.exp(teacher[0] / TEACHER_TEMP) / my_total_t
    grad_score = GRAD_SCALE * (prob_s - prob_t)
    grad_input, last_rows, grad_kv = backward_pairs(
        stored,
        grad_score,
        norm_gain,
        final_gain,
        score_vector,
        full_query,
        full_key,
        full_value,
        full_out_t.T,
    )
    grad_kv = grad_kv.astype(jnp.bfloat16)
    if own_kernels:
        spaced = jnp.pad(last_rows.reshape(pair_count * 4, -1), ((0, -pair_count * 4 % 16), (0, 0)))
        reduced, rows, losses = reduce_gradients(
            grad_kv, spaced, jnp.full((1, HEAD_WIDTH), loss_here), pb_count, neg_count
        )
        rows = rows.reshape(-1, spaced.shape[0], spaced.shape[1])[:, : pair_count * 4]
        rows = rows.reshape(pb_count * neg_count * pair_count, -1)
        loss_value = jnp.sum(losses[:, 0, 0])
    else:
        reduced = lax.psum_scatter(grad_kv, both, scatter_dimension=0, tiled=True)
        reduced = reduced.astype(jnp.float32)
        rows = lax.all_gather(last_rows, both, axis=0, tiled=True)
        loss_value = lax.psum(loss_here, "pb")
    index = row * lax.axis_size("neg") + lax.axis_index("neg")
    share = query_weight.shape[0]
    model_width = share * lax.axis_size("pb") * lax.axis_size("neg")
    out_share = out_weight.shape[1]
    normed_cols = lax.dynamic_slice_in_dim(rows, index * share, share, axis=1)
    resid_cols = lax.dynamic_slice_in_dim(rows, model_width + index * out_share, out_share, axis=1)
    rest = 2 * model_width
    all_q = rows[:, rest : rest + width]
    all_context = rows[:, rest + width :]
    grad_query = jnp.dot(normed_cols.T, all_q, preferred_element_type=jnp.float32)
    grad_out = jnp.dot(all_context.T, resid_cols, preferred_element_type=jnp.float32)
    return (
        scores_here[None],
        loss_value,
        grad_input[None],
        grad_query,
        reduced[:, :kv_width],
        reduced[:, kv_width:],
        grad_out,
    )


def solution(mesh):
    placed = (
        P("pb", "neg", None, None),
        P("pb", "neg"),
        P("pb", "neg"),
        P(),
        P(),
        P(),
        P(("pb", "neg"), None),
        P(("pb", "neg"), None),
        P(("pb", "neg"), None),
        P(None, ("pb", "neg")),
    )
    return jax.shard_map(
        shards,
        mesh=mesh,
        in_specs=placed,
        out_specs=(
            P("pb", "neg"),
            P(),
            P("pb", "neg", None, None),
            P(("pb", "neg"), None),
            P(("pb", "neg"), None),
            P(("pb", "neg"), None),
            P(None, ("pb", "neg")),
        ),
        check_vma=False,
    )
```

profile of v0, /device:TPU:0, one launch (start us, length us, event | category | flops | bytes accessed | tf_op | source)
XLA Modules:
  0.0 142.9 jit_solution(320514408100106228)
XLA Ops:
  0.7 0.8 compare_and_fusion
  1.4 0.7 add_bitcast_fusion.1
  2.1 0.7 compare_select_fusion
  2.8 1.5 %multiply_reduce_fusion = f32[4,128]{1,0:T(4,128)S(1)} fusion(bf16[1,4,128,1024]{3,2,1,0:T(8,128)(2,1)} %param.10), kind=kLoop, calls=%fused_computation.21 | loop fusion | flops 1572352 | bytes 1050624 | tf_op jit(solution)/shard_map/reduce_sum | solution.py:53
  4.3 0.6 fusion.64
  4.9 0.7 fusion.47
  5.6 1.0 fusion.48
  6.6 1.0 fusion.49
  7.6 0.9 broadcast_multiply_fusion.3
  8.4 1.0 multiply_convert_fusion
  9.5 0.6 gather_fusion.1
  10.1 0.7 broadcast_select_fusion
  10.8 0.2 convert_bitcast_fusion
  11.0 1.2 gather_fusion
  12.2 39.4 %shard_map.153 = (bf16[1024,1024]{1,0:T(8,128)(2,1)S(1)}, bf16[1024,512]{1,0:T(8,128)(2,1)S(1)}, bf16[1024,512]{1,0:T(8,128)(2,1)S(1)}, bf16[1024,1024]{1,0:T(8,128)(2,1)S(1)}) custom-call(bf16[32,1024]{1,0:T(8,128)(2,1)S(1)} %copy-done.3, bf16[32,512]{1,0:T(8,128)(2,1)S(1)} %copy-done.5, bf16[32,512]{1,0:T(8,128)(2,1)S(1)} %copy-done.6, ...), custom_call_target="tpu_custom_call" | custom-call | tf_op jit(solution)/shard_map/pallas_call | solution.py:415
  51.7 1.3 copy-done
  53.0 1.0 copy-done.1
  54.0 1.3 copy.40
  55.3 3.1 %convolution_convert_fusion.2 = bf16[4,128,4,128]{3,1,2,0:T(8,128)(2,1)} fusion(bf16[4,128,1024,1]{2,1,0,3:T(8,128)(2,1)} %bitcast.145, bf16[1,4,128,1024]{3,2,1,0:T(8,128)(2,1)} %param.10, f32[1024]{0:T(1024)S(1)} %copy-done.16, f32[4,128]{1,0:T(4,128)} %copy-done.20), kind=kOutput, calls=%fused_computation.26 | convolution fusion | flops 539230208 | bytes 2627584 | tf_op jit(solution)/shard_map/dot_general | solution.py:59
  58.4 2.3 %copy.39 = bf16[512,1024]{1,0:T(8,128)(2,1)} copy(bf16[512,1024]{0,1:T(8,128)(2,1)} %bitcast.135) | data formatting | bytes 2097152 | tf_op jit(solution)/shard_map/dot_general | solution.py:56
  60.7 2.4 %multiply_reduce_fusion.2 = (f32[4,128,4]{1,2,0:T(4,128)S(1)}, f32[4,128,4,128]{1,3,2,0:T(8,128)S(1)}) fusion(bf16[4,128,1024,1]{2,1,0,3:T(8,128)(2,1)} %bitcast.144, bf16[1,4,128,1024]{3,2,1,0:T(8,128)(2,1)} %param.10, f32[1024]{0:T(1024)S(1)} %copy-done.16, f32[4,128]{1,0:T(4,128)S(1)} %copy-done.21), kind=kOutput, calls=%fused_computation.45 | convolution fusion | flops 539490304 | bytes 3160064 | tf_op jit(solution)/shard_map/dot_general | solution.py:56
  63.1 0.1 broadcast_multiply_fusion.1
  63.2 0.1 slice_negate_fusion.1
  63.3 0.7 copy-done.9
  64.0 1.0 fusion.19
  65.0 2.6 %copy.38 = bf16[1024,1024]{1,0:T(8,128)(2,1)} copy(bf16[1024,1024]{0,1:T(8,128)(2,1)S(1)} %bitcast.133) | data formatting | bytes 4194304 | tf_op jit(solution)/shard_map/dot_general | solution.py:66
  67.7 2.4 %multiply_reduce_fusion.8 = (f32[4,8]{0,1:T(8,128)S(1)}, f32[4,8,128]{2,0,1:T(4,128)S(1)}) fusion(bf16[8,128,1024]{2,1,0:T(8,128)(2,1)} %bitcast.139, bf16[4,1024]{1,0:T(4,128)(2,1)S(1)} %gather_fusion.1, pred[4]{0:T(512)(128)(4,1)S(1)} %copy-done.28), kind=kOutput, calls=%fused_computation.83 | convolution fusion | flops 8400864 | bytes 2121860 | tf_op jit(solution)/shard_map/dot_general | solution.py:66
  70.3 0.1 fusion.35
  70.4 0.2 fusion.16
  70.6 1.4 convolution_convert_fusion.4
  72.0 2.4 %multiply_reduce_fusion.7 = (f32[4]{0:T(128)S(1)}, f32[4,1024]{1,0:T(4,128)S(1)}) fusion(bf16[4,1024]{1,0:T(4,128)(2,1)S(1)} %reshape.387, bf16[1024,1024]{1,0:T(8,128)(2,1)} %copy-done, f32[4,1024]{1,0:T(4,128)S(1)} %copy-done.15, pred[4]{0:T(512)(128)(4,1)S(1)} %copy-done.28), kind=kOutput, calls=%fused_computation.82 | convolution fusion | flops 8404988 | bytes 2138132 | tf_op jit(solution)/shard_map/dot_general | solution.py:95
  74.4 0.2 multiply_reduce_fusion.6
  74.7 0.5 pad.4.own
  75.2 8.0 %shard_map.154 = f32[8,1,128]{2,1,0:T(1,128)} custom-call(f32[1,128]{1,0:T(1,128)} %pad.4.own), custom_call_target="tpu_custom_call" | custom-call | tf_op jit(solution)/shard_map/pallas_call | solution.py:454
  83.2 1.4 %exponential_reduce_fusion = (f32[]{:T(128)}, f32[]{:T(128)}) fusion(f32[8,8]{1,0:T(8,128)} %bitcast.146), kind=kLoop, calls=%fused_computation.98 | loop fusion | flops 94 | bytes 264 | tf_op jit(solution)/shard_map/reduce_sum | solution.py:650
  86.0 2.1 %multiply_reduce_fusion.9 = f32[]{:T(128)} fusion(f32[8,8]{1,0:T(8,128)} %bitcast.147, f32[]{:T(128)S(6)} %log.7, f32[]{:T(128)S(6)} %log.6, f32[]{:T(128)} %get-tuple-element.22), kind=kLoop, calls=%fused_computation.96 | loop fusion | flops 223 | bytes 272 | tf_op jit(solution)/shard_map/reduce_sum | solution.py:653
  88.1 1.3 fusion.56
  89.4 0.6 broadcast_in_dim.45.loss_row
  90.1 0.2 multiply_reduce_fusion.5
  90.4 2.0 %convolution_convert_fusion.3 = bf16[4,1024]{1,0:T(4,128)(2,1)S(1)} fusion(bf16[4,1024]{1,0:T(4,128)(2,1)S(1)} %get-tuple-element.23, bf16[1024,1024]{1,0:T(8,128)(2,1)} %copy-done), kind=kOutput, calls=%fused_computation.33 | convolution fusion | flops 8392704 | bytes 2113536 | tf_op jit(solution)/shard_map/dot_general | solution.py:169
  92.4 1.4 fusion.70
  93.8 0.2 multiply_reduce_fusion.4
  94.0 0.1 multiply_convert_fusion.3
  94.1 1.4 convolution_multiply_fusion
  95.7 0.2 multiply_reduce_fusion.3
  95.9 0.6 fusion.71
  96.7 0.4 fusion.14
  97.1 1.1 copy.32
  98.2 0.4 broadcast_multiply_fusion
  98.6 0.8 copy-done.10
  99.4 0.3 multiply_reduce_fusion.1
  99.7 1.1 multiply_convert_fusion.1
  100.9 2.1 %copy.31 = bf16[4,128,4,128]{3,2,1,0:T(4,128)(2,1)} copy(bf16[4,128,4,128]{1,3,2,0:T(8,128)(2,1)} %multiply_convert_fusion.1) | data formatting | bytes 1048576 | tf_op jit(solution)/shard_map/convert_element_type | solution.py:202
  103.0 1.9 %fusion.65 = f32[512,1024]{1,0:T(8,128)S(1)} fusion(bf16[1024,512]{1,0:T(8,128)(2,1)S(1)} %copy-done.2, bf16[64,8,4,128]{3,2,1,0:T(4,128)(2,1)} %bitcast.142), kind=kOutput, calls=%fused_computation.138 | convolution fusion | flops 536870912 | bytes 3670016 | tf_op jit(solution)/shard_map/dot_general | solution.py:215
  104.9 1.2 fusion.3
  106.2 2.5 %fusion.11 = bf16[1,4,128,1024]{3,2,1,0:T(8,128)(2,1)} fusion(bf16[1,4,128,1024]{3,2,1,0:T(8,128)(2,1)S(1)} %copy-done.8, f32[1,4,128,1024]{3,2,1,0:T(8,128)S(1)} %bitcast.138, f32[4,1024]{1,0:T(4,128)S(1)} %get-tuple-element.24, f32[4,128]{1,0:T(4,128)S(1)} %multiply_bitcast_fusion, f32[4,1024]{1,0:T(4,128)S(1)} %fusion.71, f32[4,128]{1,0:T(4,128)S(1)} %copy-done.23, ...), kind=kLoop, calls=%fused_computation.17 | loop fusion | flops 6815744 | bytes 4237312 | tf_op jit(solution)/shard_map/convert_element_type | solution.py:228
  108.6 0.1 copy_bitcast_fusion
  108.8 1.3 convolution_convert_fusion
  110.1 29.0 %shard_map.155 = (f32[32,1024]{1,0:T(8,128)S(1)}, bf16[512,1024]{1,0:T(8,128)(2,1)S(1)}, f32[4,1,128]{2,1,0:T(1,128)S(1)}) custom-call(bf16[4,4,2,32,1024]{4,3,2,1,0:T(8,128)(2,1)S(1)} %bitcast.136, bf16[16,1024]{1,0:T(8,128)(2,1)S(1)} %reshape.391.last_rows, f32[1,128]{1,0:T(1,128)S(1)} %broadcast_in_dim.45.loss_row), custom_call_target="tpu_custom_call" | custom-call | tf_op jit(solution)/shard_map/pallas_call | solution.py:569
  139.1 0.6 slice_reduce_fusion
  139.7 0.7 fusion.68
  140.4 0.7 reshape_reshape.3
  141.0 0.9 fusion.28
  142.0 0.9 fusion.26
  (86 shorter events, 1.1 us)
Async XLA Ops:
  0.6 7.8 %copy-start.7 = (bf16[1,4,128,1024]{3,2,1,0:T(8,128)(2,1)S(1)}, bf16[1,4,128,1024]{3,2,1,0:T(8,128)(2,1)}, u32[]{:S(2)}) copy-start(bf16[1,4,128,1024]{3,2,1,0:T(8,128)(2,1)} %param.10) | copy-start | bytes 3145732
  1.4 8.7 %copy-start.27 = (pred[4]{0:T(512)(128)(4,1)}, pred[4]{0:T(512)(128)(4,1)S(1)}, u32[]{:S(2)}) copy-start(pred[4]{0:T(512)(128)(4,1)S(1)} %compare_and_fusion) | copy-start | bytes 16
  4.9 3.6 %copy-start.20 = (f32[4,128]{1,0:T(4,128)}, f32[4,128]{1,0:T(4,128)S(1)}, u32[]{:S(2)}) copy-start(f32[4,128]{1,0:T(4,128)S(1)} %get-tuple-element.42) | copy-start | bytes 6148
  9.4 2.8 %copy-start.3 = (bf16[32,1024]{1,0:T(8,128)(2,1)S(1)}, bf16[32,1024]{1,0:T(8,128)(2,1)}, u32[]{:S(2)}) copy-start(bf16[32,1024]{1,0:T(8,128)(2,1)} %refs_0_.1) | copy-start | bytes 196612
  9.5 2.8 %copy-start.4 = (bf16[1024,32]{0,1:T(8,128)(2,1)S(1)}, bf16[1024,32]{0,1:T(8,128)(2,1)}, u32[]{:S(2)}) copy-start(bf16[1024,32]{0,1:T(8,128)(2,1)} %param.19) | copy-start | bytes 196612
  9.5 2.8 %copy-start.5 = (bf16[32,512]{1,0:T(8,128)(2,1)S(1)}, bf16[32,512]{1,0:T(8,128)(2,1)}, u32[]{:S(2)}) copy-start(bf16[32,512]{1,0:T(8,128)(2,1)} %refs_1_.1) | copy-start | bytes 98308
  9.5 2.7 %copy-start.6 = (bf16[32,512]{1,0:T(8,128)(2,1)S(1)}, bf16[32,512]{1,0:T(8,128)(2,1)}, u32[]{:S(2)}) copy-start(bf16[32,512]{1,0:T(8,128)(2,1)} %refs_2_.1) | copy-start | bytes 98308
  10.8 44.5 %copy-start.16 = (f32[1024]{0:T(1024)S(1)}, f32[1024]{0:T(1024)}, u32[]{:S(2)}) copy-start(f32[1024]{0:T(1024)} %param.13) | copy-start | bytes 12292
  51.7 1.3 copy-start
  53.0 1.0 copy-start.1
  55.3 5.4 %copy-start.21 = (f32[4,128]{1,0:T(4,128)S(1)}, f32[4,128]{1,0:T(4,128)}, u32[]{:S(2)}) copy-start(f32[4,128]{1,0:T(4,128)} %copy-done.20) | copy-start | bytes 6148
  63.0 1.0 copy-start.9
  63.1 0.9 copy-start.14
  65.0 2.6 %copy-start.28 = (pred[4]{0:T(512)(128)(4,1)S(1)}, pred[4]{0:T(512)(128)(4,1)}, u32[]{:S(2)}) copy-start(pred[4]{0:T(512)(128)(4,1)} %copy-done.27) | copy-start | bytes 16
  67.6 2.6 %copy-start.25 = (f32[4,128]{1,0:T(4,128)S(1)}, f32[4,128]{1,0:T(4,128)}, u32[]{:S(2)}) copy-start(f32[4,128]{1,0:T(4,128)} %fusion.49) | copy-start | bytes 6148
  67.6 2.6 %copy-start.26 = (f32[4,128]{1,0:T(4,128)S(1)}, f32[4,128]{1,0:T(4,128)}, u32[]{:S(2)}) copy-start(f32[4,128]{1,0:T(4,128)} %fusion.48) | copy-start | bytes 6148
  67.6 2.7 %copy-start.13 = (bf16[4,128,4,128]{1,3,2,0:T(8,128)(2,1)S(1)}, bf16[4,128,4,128]{1,3,2,0:T(8,128)(2,1)}, u32[]{:S(2)}) copy-start(bf16[4,128,4,128]{1,3,2,0:T(8,128)(2,1)} %fusion.19) | copy-start | bytes 1572868
  67.6 2.7 %copy-start.29 = (pred[4,128]{1,0:T(4,128)(4,1)S(1)}, pred[4,128]{1,0:T(4,128)(4,1)}, u32[]{:S(2)}) copy-start(pred[4,128]{1,0:T(4,128)(4,1)} %get-tuple-element.45) | copy-start | bytes 1540
  67.6 4.3 %copy-start.15 = (f32[4,1024]{1,0:T(4,128)S(1)}, f32[4,1024]{1,0:T(4,128)}, u32[]{:S(2)}) copy-start(f32[4,1024]{1,0:T(4,128)} %gather_fusion) | copy-start | bytes 49156
  70.0 4.3 %copy-start.17 = (f32[1024]{0:T(1024)S(1)}, f32[1024]{0:T(1024)}, u32[]{:S(2)}) copy-start(f32[1024]{0:T(1024)} %param.15) | copy-start | bytes 12292
  70.0 4.4 %copy-start.18 = (f32[1024]{0:T(1024)S(1)}, f32[1024]{0:T(1024)}, u32[]{:S(2)}) copy-start(f32[1024]{0:T(1024)} %param.14) | copy-start | bytes 12292
  70.1 4.5 %copy-start.31 = (f32[1,4]{1,0:T(1,128)S(1)}, f32[1,4]{1,0:T(1,128)}, u32[]{:S(2)}) copy-start(f32[1,4]{1,0:T(1,128)} %param.12) | copy-start | bytes 52
  74.6 22.0 %copy-start.30 = (f32[4]{0:T(128)}, f32[4]{0:T(128)S(1)}, u32[]{:S(2)}) copy-start(f32[4]{0:T(128)S(1)} %multiply_reduce_fusion.6) | copy-start | bytes 52
  92.3 4.2 %copy-start.19 = (bf16[4,1024]{1,0:T(4,128)(2,1)S(1)}, bf16[4,1024]{1,0:T(4,128)(2,1)}, u32[]{:S(2)}) copy-start(bf16[4,1024]{1,0:T(4,128)(2,1)} %broadcast_select_fusion) | copy-start | bytes 24580
  98.2 1.2 copy-start.10
  99.7 3.3 %copy-start.2 = (bf16[1024,512]{1,0:T(8,128)(2,1)S(1)}, bf16[1024,512]{1,0:T(8,128)(2,1)}, u32[]{:S(2)}) copy-start(bf16[1024,512]{1,0:T(8,128)(2,1)} %copy-done.1) | copy-start | bytes 3145732
  103.0 1.9 %copy-start.8 = (bf16[1,4,128,1024]{3,2,1,0:T(8,128)(2,1)S(1)}, bf16[1,4,128,1024]{3,2,1,0:T(8,128)(2,1)}, u32[]{:S(2)}) copy-start(bf16[1,4,128,1024]{3,2,1,0:T(8,128)(2,1)} %param.10) | copy-start | bytes 3145732
  103.0 1.9 %copy-start.11 = (bf16[4,128,4,128]{3,2,1,0:T(4,128)(2,1)S(1)}, bf16[4,128,4,128]{3,2,1,0:T(4,128)(2,1)}, u32[]{:S(2)}) copy-start(bf16[4,128,4,128]{3,2,1,0:T(4,128)(2,1)} %copy.32) | copy-start | bytes 1572868
  103.0 1.9 %copy-start.22 = (f32[512]{0:T(512)S(1)}, f32[512]{0:T(512)}, u32[]{:S(2)}) copy-start(f32[512]{0:T(512)} %get-tuple-element.41) | copy-start | bytes 6148
  103.0 2.0 %copy-start.24 = (f32[512]{0:T(512)S(1)}, f32[512]{0:T(512)}, u32[]{:S(2)}) copy-start(f32[512]{0:T(512)} %get-tuple-element.44) | copy-start | bytes 6148
  104.9 1.2 copy-start.23
  106.2 2.5 %copy-start.12 = (bf16[4,128,4,128]{3,2,1,0:T(4,128)(2,1)S(1)}, bf16[4,128,4,128]{3,2,1,0:T(4,128)(2,1)}, u32[]{:S(2)}) copy-start(bf16[4,128,4,128]{3,2,1,0:T(4,128)(2,1)} %copy.31) | copy-start | bytes 1572868
where the time goes:
time: 144 us; the launch traced here: 143 us
  Pallas kernels  76.4 us (53%)
  matrix products  26.2 us (18%)
  other arithmetic  20 us (14%)
  local copies, waits for them, and re-layouts  17.8 us (12%)
  between operations  2.54 us (2%)
    pallas_call x1, Pallas kernels, gather_weights(): pl.pallas_call(functools.partial(gather_kernel, count), out_shape=tuple((...  39.4 us
    pallas_call x1, Pallas kernels, reduce_gradients(): pl.pallas_call(reduce_kernel, out_shape=(jax.ShapeDtypeStruct((share, wid...  29 us
    pallas_call x1, Pallas kernels, exchange_listing(): pl.pallas_call(listing_kernel, out_shape=jax.ShapeDtypeStruct((neg_count,...  8.01 us
    unnamed x65, local copies, waits for them, and re-layouts  3.94 us
    dot_general x1, matrix products, forward_pairs(): jnp.dot(flat_rows, value_matrix, preferred_element_type=jnp.float32)  3.11 us

commit v1 on v0

--- a/solution.py
+++ b/solution.py
@@ -2,6 +2,7 @@
 
 import jax
 import jax.numpy as jnp
+import numpy as np
 from jax import lax
 from jax.experimental import pallas as pl
 from jax.experimental.pallas import tpu as pltpu
@@ -22,6 +23,15 @@
     angles = jnp.arange(seq_len, dtype=jnp.float32)[:, None] * freqs[None, :]
     angles = jnp.concatenate([angles, angles], axis=1)
     return (jnp.cos(angles), jnp.sin(angles))
+
+
+def signed_tables(seq_len, head_size):
+    half = head_size // 2
+    freqs = ROPE_BASE ** (-(np.arange(half) * 2.0) / head_size)
+    angles = np.arange(seq_len)[:, None] * freqs[None, :]
+    cos = np.concatenate([np.cos(angles)] * 2, axis=1)
+    sin = np.concatenate([-np.sin(angles), np.sin(angles)], axis=1)
+    return (jnp.asarray(cos, jnp.float32), jnp.asarray(sin, jnp.float32))
 
 
 def rotate_half(vector):
@@ -353,8 +363,8 @@
             self.spread(block, line)
 
     def half(self, block, side):
-        width = block.shape[1] // 2
-        return block.at[:, pl.ds(side * width, width)]
+        size = block.shape[0] // 2
+        return block.at[pl.ds(side * size, size)]
 
     def relay(self):
         at = self.place
@@ -384,113 +394,418 @@
         for pb in range(at.pb_count):
             for line in range(at.line_count):
                 self.arrive(self.rows(pb, line, at.partner), self.core_recv.at[pb, line])
+        self.local.wait()
+
+    def drain(self):
         for copy in self.sent:
             copy.wait_send()
-        self.local.wait()
-
-
-def gather_kernel(count, *refs):
-    place = Place()
-    place.greet()
-    owns, fulls, sems = refs[:count], refs[count : 2 * count], refs[2 * count :]
-    each = len(sems) // count
-    gathers = [
-        Gather(place, owns[i], fulls[i], sems[i * each : (i + 1) * each]) for i in range(count)
-    ]
-    for gather in gathers:
-        gather.start()
-    for gather in gathers:
-        gather.middle()
-    for gather in gathers:
-        gather.relay()
-    for gather in gathers:
-        gather.finish()
 
 
 VMEM_SPEC = pl.BlockSpec(memory_space=pltpu.VMEM)
 
 
-def gather_weights(shares, pb_count, neg_count):
-    count = len(shares)
-    return pl.pallas_call(
-        functools.partial(gather_kernel, count),
-        out_shape=tuple(
-            jax.ShapeDtypeStruct((w.shape[0] * pb_count * neg_count, w.shape[1]), w.dtype)
-            for w in shares
-        ),
-        in_specs=[VMEM_SPEC] * count,
-        out_specs=(VMEM_SPEC,) * count,
-        scratch_shapes=gather_sems(pb_count, neg_count) * count,
-        compiler_params=pltpu.CompilerParams(
-            collective_id=0, has_side_effects=True, vmem_limit_bytes=32 * 2**20
-        ),
-    )(*shares)
-
-
-def listing_kernel(own, full, send, recv, local_sem):
-    at = Place()
-    barrier = pltpu.get_barrier_semaphore()
-    neg = lax.axis_index("neg")
-    peers = [lax.rem(neg + k, at.neg_count) for k in range(1, at.neg_count)]
-    for peer in peers:
-        pl.semaphore_signal(barrier, inc=1, device_id=(at.pb, peer), device_id_type=MESH_ID)
-    pl.semaphore_wait(barrier, len(peers))
-    copies = []
-    local = pltpu.make_async_copy(own, full.at[neg], local_sem)
-    local.start()
-    for k, peer in enumerate(peers):
-        copy = remote(own, full.at[neg], send.at[k], recv.at[neg], (at.pb, peer))
-        copy.start()
-        copies.append(copy)
-    local.wait()
-    for peer in peers:
-        block = full.at[peer]
-        remote(block, block, local_sem, recv.at[peer], (at.pb, peer)).wait_recv()
-    for copy in copies:
-        copy.wait_send()
-
-
-def exchange_listing(own, neg_count):
-    return pl.pallas_call(
-        listing_kernel,
-        out_shape=jax.ShapeDtypeStruct((neg_count,) + own.shape, own.dtype),
-        in_specs=[VMEM_SPEC],
-        out_specs=VMEM_SPEC,
-        scratch_shapes=[
-            pltpu.SemaphoreType.DMA((neg_count,)),
-            pltpu.SemaphoreType.DMA((neg_count,)),
-            pltpu.SemaphoreType.DMA,
-        ],
-        compiler_params=pltpu.CompilerParams(collective_id=1, has_side_effects=True),
-    )(own)
-
-
-def reduce_kernel(
+def mm(left, right, left_dim=1, right_dim=0, precision=None):
+    return lax.dot_general(
+        left,
+        right,
+        (((left_dim,), (right_dim,)), ((), ())),
+        preferred_element_type=jnp.float32,
+        precision=precision,
+    )
+
+
+def lane_mean(array):
+    return jnp.mean(array, axis=-1, keepdims=True)
+
+
+def tile(array, index):
+    return array[:, index * HEAD_WIDTH : (index + 1) * HEAD_WIDTH]
+
+
+class Exchange:
+    def __init__(self, at, src, dst, send_sem, recv_sem):
+        self.at, self.src, self.dst = at, src, dst
+        self.send_sem, self.recv_sem = send_sem, recv_sem
+
+    def start(self):
+        at = self.at
+
+        def one(step, carry):
+            peer = lax.rem(at.me + step, at.count)
+            target = (peer // at.neg_count, lax.rem(peer, at.neg_count))
+            remote(
+                self.src.at[peer], self.dst.at[at.me], self.send_sem, self.recv_sem, target
+            ).start()
+            return carry
+
+        lax.fori_loop(1, at.count, one, 0)
+        self.dst[at.me] = self.src[at.me]
+
+    def wait(self, sem_of):
+        block = self.dst.at[pl.ds(0, self.at.count - 1)]
+        copy = remote(block, block, self.send_sem, self.recv_sem, self.at.to_partner())
+        getattr(copy, sem_of)()
+
+
+def step_kernel(
+    sizes,
+    x,
+    lengths,
+    teacher,
+    norm_gain,
+    final_gain,
+    score_vector,
+    cos_table,
+    sin_table,
+    own_q,
+    own_k,
+    own_v,
+    own_out,
+    scores_out,
+    loss_out,
+    grad_hidden,
+    grad_query,
+    grad_key,
+    grad_value,
+    grad_out,
+    own_o,
+    full_q,
+    full_k,
+    full_v,
+    full_o,
+    normed,
+    inv_wide,
+    key_unit,
+    key_scale,
+    key_rot,
+    value_cast,
+    grad_k,
+    grad_v,
+    logit_grad,
+    probs_ref,
+    query_blocks,
+    context_blocks,
+    last_grad,
+    resid_grad,
+    context_own,
+    context_full,
+    late_own,
+    late_full,
+    early_src,
+    early_dst,
+    resid_src,
+    resid_dst,
+    list_src,
+    list_dst,
     partial,
-    last_rows,
-    loss_row,
-    reduced,
-    all_rows,
-    all_losses,
     from_core,
     paired,
     from_pb,
     summed,
     from_line,
+    early_sems,
+    resid_sems,
+    list_sems,
     core_send,
     core_recv,
     pb_send,
     pb_recv,
     line_send,
     line_recv,
-    loss_send,
-    loss_recv,
-    loss_local,
-    *sems,
+    any_sem,
+    *gather_sem_refs,
 ):
+    pairs, seq, groups, share = sizes
+    bf16, f32 = jnp.bfloat16, jnp.float32
     at = Place()
-    at.greet()
-    gather = Gather(at, last_rows, all_rows, sems)
+    at.count = at.pb_count * at.neg_count
+    at.me = at.slot(at.pb, at.line, at.core)
+    model = x.shape[1]
+    rows_all = pairs * seq
+    per_group = own_q.shape[1] // own_k.shape[1]
+    slots = per_group * pairs
+    stacked = groups * slots
+    kv_width = groups * HEAD_WIDTH
+
+    barrier = pltpu.get_barrier_semaphore()
+
+    def greet(step, carry):
+        peer = lax.rem(at.me + step, at.count)
+        target = (peer // at.neg_count, lax.rem(peer, at.neg_count))
+        pl.semaphore_signal(barrier, inc=1, device_id=target, device_id_type=MESH_ID)
+        return carry
+
+    lax.fori_loop(1, at.count, greet, 0)
+
+    each = len(gather_sem_refs) // 6
+    gathers = []
+    for place_of, (own, full) in enumerate(
+        (
+            (own_k, full_k),
+            (own_v, full_v),
+            (own_q, full_q),
+            (own_o, full_o),
+            (context_own, context_full),
+            (late_own, late_full),
+        )
+    ):
+        sems = gather_sem_refs[place_of * each : (place_of + 1) * each]
+        gathers.append(Gather(at, own, full, sems))
+    gather_k, gather_v, gather_q, gather_o, gather_context, gather_late = gathers
+
+    diagonal = lax.broadcasted_iota(jnp.int32, (share, share), 0) == lax.broadcasted_iota(
+        jnp.int32, (share, share), 1
+    )
+    own_o[...] = mm(diagonal.astype(f32).astype(bf16), own_out[...], 1, 1).astype(bf16)
+
+    pl.semaphore_wait(barrier, at.count - 1)
+    gather_k.start()
+    gather_v.start()
+    gather_q.start()
+    gather_o.start()
+
+    def norm_pair(pair, carry):
+        rows = pl.ds(pl.multiple_of(pair * seq, seq), seq)
+        wide = x[rows, :].astype(f32)
+        inv = lax.rsqrt(lane_mean(wide * wide) + EPSILON)
+        inv_wide[rows, :] = jnp.broadcast_to(inv, (seq, HEAD_WIDTH))
+        normed[rows, :] = (wide * inv * norm_gain[...]).astype(bf16)
+        return carry
+
+    lax.fori_loop(0, pairs, norm_pair, 0)
+
+    row8 = lax.broadcasted_iota(jnp.int32, (slots, 1), 0)
+    pair8 = lax.rem(row8, pairs)
+    upper8 = row8 < pairs
+    last8 = jnp.zeros((slots, 1), jnp.int32)
+    teacher8 = jnp.zeros((slots, 1), f32)
+    for pair in range(pairs):
+        last8 = jnp.where(pair8 == pair, lengths[0, pair] - 1, last8)
+        teacher8 = jnp.where(pair8 == pair, teacher[0, pair], teacher8)
+    place8 = pair8 * seq + last8
+    column8 = lax.broadcasted_iota(jnp.int32, (slots, rows_all), 1)
+    onehot8 = (column8 == place8).astype(f32).astype(bf16)
+    visible8 = (column8 >= pair8 * seq) & (column8 <= place8)
+    visible = jnp.concatenate([visible8.astype(f32)] * groups, axis=0) > 0.5
+    position8 = (lax.broadcasted_iota(jnp.int32, (slots, seq), 1) == last8).astype(f32)
+
+    gather_k.middle()
+    gather_v.middle()
+    gather_k.relay()
+
+    x_last = mm(onehot8, x[...])
+    normed_last = mm(onehot8, normed[...]).astype(bf16)
+    cos8 = mm(position8, cos_table[...], precision=lax.Precision.HIGHEST)
+    sin8 = mm(position8, sin_table[...], precision=lax.Precision.HIGHEST)
+    cos_rows = jnp.concatenate([cos8] * groups, axis=0)
+    sin_rows = jnp.concatenate([sin8] * groups, axis=0)
+
+    gather_q.middle()
+    gather_v.relay()
+    gather_k.finish()
+
+    def key_pair(pair, carry):
+        rows = pl.ds(pl.multiple_of(pair * seq, seq), seq)
+        proj = mm(normed[rows, :], full_k[...])
+        for group in range(groups):
+            lanes = slice(group * HEAD_WIDTH, (group + 1) * HEAD_WIDTH)
+            part = proj[:, lanes]
+            scale = lax.rsqrt(lane_mean(part * part) + EPSILON)
+            unit = part * scale
+            key_unit[rows, lanes] = unit
+            key_scale[rows, lanes] = jnp.broadcast_to(scale, (seq, HEAD_WIDTH))
+            turned = unit * cos_table[...] + pltpu.roll(unit, HEAD_WIDTH // 2, 1) * sin_table[...]
+            key_rot[rows, lanes] = turned.astype(bf16)
+        return carry
+
+    lax.fori_loop(0, pairs, key_pair, 0)
+
+    gather_o.middle()
+    gather_q.relay()
+    gather_v.finish()
+
+    def value_pair(pair, carry):
+        rows = pl.ds(pl.multiple_of(pair * seq, seq), seq)
+        value_cast[rows, :] = mm(normed[rows, :], full_v[...]).astype(bf16)
+        return carry
+
+    lax.fori_loop(0, pairs, value_pair, 0)
+
+    gather_o.relay()
+    gather_q.finish()
+
+    def stack_heads(wide):
+        return jnp.concatenate(
+            [
+                jnp.where(upper8, tile(wide, per_group * group), tile(wide, per_group * group + 1))
+                for group in range(groups)
+            ],
+            axis=0,
+        )
+
+    def spread_heads(stack):
+        parts = []
+        for group in range(groups):
+            part = stack[group * slots : (group + 1) * slots]
+            parts += [jnp.where(upper8, part, 0.0), jnp.where(upper8, 0.0, part)]
+        return jnp.concatenate(parts, axis=1).astype(bf16)
+
+    def diagonal_of(wide):
+        return jnp.concatenate(
+            [
+                wide[group * slots : (group + 1) * slots, group * HEAD_WIDTH : (group + 1) * HEAD_WIDTH]
+                for group in range(groups)
+            ],
+            axis=0,
+        )
+
+    def blocks_of(stack):
+        rows = []
+        for group in range(groups):
+            part = stack[group * slots : (group + 1) * slots]
+            rows.append(
+                jnp.concatenate(
+                    [part if other == group else jnp.zeros_like(part) for other in range(groups)],
+                    axis=1,
+                )
+            )
+        return jnp.concatenate(rows, axis=0).astype(bf16)
+
+    query_proj = stack_heads(mm(normed_last, full_q[...]))
+    query_scale = lax.rsqrt(lane_mean(query_proj * query_proj) + EPSILON)
+    query_unit = query_proj * query_scale
+    query_rot = query_unit * cos_rows + pltpu.roll(query_unit, HEAD_WIDTH // 2, 1) * sin_rows
+    query_wide = blocks_of(query_rot)
+    query_blocks[...] = query_wide
+    logits = mm(query_wide, key_rot[...], 1, 1) * HEAD_WIDTH ** (-0.5)
+    expos = jnp.where(visible, jnp.exp(logits), 0.0)
+    attention_weights = expos / jnp.sum(expos, axis=-1, keepdims=True)
+    probs = attention_weights.astype(bf16)
+    probs_ref[...] = probs
+    context = diagonal_of(mm(probs, value_cast[...]))
+    context_own[...] = context.astype(bf16)
+    context_wide = spread_heads(context)
+
+    lane_block = lax.rem(
+        lax.broadcasted_iota(jnp.int32, (slots, model), 1) // share, HEAD_WIDTH // share
+    )
+
+    def pack(parts, turn):
+        total = jnp.zeros((slots, model), f32)
+        for block, part in enumerate(parts):
+            shift = ((block - turn) * share) % model
+            moved = part if shift == 0 else pltpu.roll(part, shift, 1)
+            total = jnp.where(lane_block == block, moved, total)
+        return total
+
+    def by_head(wide):
+        return [jnp.where(upper8, wide, 0.0), jnp.where(upper8, 0.0, wide)]
+
+    turns = HEAD_WIDTH // share
+    pulled = mm(probs, normed[...])
+    pulled_parts = [pulled[group * slots : (group + 1) * slots] for group in range(groups)]
+    last_parts = by_head(normed_last.astype(f32))
+    for turn in range(turns):
+        both = jnp.concatenate([pack(pulled_parts, turn), pack(last_parts, turn)], axis=0)
+        both = both.astype(bf16)
+        for index in range(model // HEAD_WIDTH):
+            early_src[index * turns + turn] = tile(both, index)
+
+    gather_o.finish()
+    attended = mm(context_wide, full_o[...], 1, 1)
+    attended = attended + pltpu.roll(attended, pairs, 0)
+    residual = x_last + attended
+    out_scale = lax.rsqrt(lane_mean(residual * residual) + EPSILON)
+    out_unit = residual * out_scale
+    gain = final_gain[...] * score_vector[...]
+    score8 = jnp.sum(out_unit * gain, axis=-1, keepdims=True)
+
+    lane8 = lax.broadcasted_iota(jnp.int32, (slots, HEAD_WIDTH), 1)
+    listing = jnp.where(lane8 == 0, score8, jnp.where(lane8 == 1, teacher8, 0.0))
+    list_src[...] = listing
+    me_tile = list_dst.at[at.me]
+    list_here, list_there, list_sent = list_sems.at[0], list_sems.at[1], list_sems.at[2]
+    neg = lax.axis_index("neg")
+
+    def list_near(step, carry):
+        peer = lax.rem(neg + step, at.neg_count)
+        remote(list_src, me_tile, list_sent, list_here, (at.pb, peer)).start()
+        return carry
+
+    def list_far(step, carry):
+        peer = lax.rem(neg + step, at.neg_count)
+        for k in range(1, at.pb_count):
+            remote(list_src, me_tile, list_sent, list_there, (at.pb_peer(k), peer)).start()
+        return carry
+
+    lax.fori_loop(1, at.neg_count, list_near, 0)
+    lax.fori_loop(0, at.neg_count, list_far, 0)
+    list_dst[at.me] = listing
+    early = Exchange(at, early_src, early_dst, early_sems.at[0], early_sems.at[1])
+    gather_context.start()
+    early.start()
+
+    row_lane = lax.broadcasted_iota(jnp.int32, (slots, HEAD_WIDTH), 0)
+    score_row = jnp.sum(jnp.where(row_lane == lane8, score8, 0.0), axis=0, keepdims=True)
+    scores_out[...] = score_row[:, :pairs]
+
+    near_block = list_dst.at[pl.ds(0, at.neg_count - 1)]
+    remote(near_block, near_block, list_sent, list_here, at.to_partner()).wait_recv()
+
+    real3 = lax.broadcasted_iota(jnp.int32, (at.neg_count, slots, 1), 1) < pairs
+    lane3 = lax.broadcasted_iota(jnp.int32, (at.neg_count, slots, HEAD_WIDTH), 2)
+
+    def query_terms(block):
+        score = jnp.sum(jnp.where(lane3 == 0, block, 0.0), axis=-1, keepdims=True)
+        scaled = jnp.sum(jnp.where(lane3 == 1, block, 0.0), axis=-1, keepdims=True) / TEACHER_TEMP
+        total = lambda array: jnp.sum(
+            jnp.sum(jnp.where(real3, array, 0.0), axis=0), axis=0, keepdims=True
+        )
+        expo_t = jnp.exp(scaled)
+        return score, scaled, expo_t, total(jnp.exp(score)), total(expo_t), total
+
+    here = list_dst[pl.ds(pl.multiple_of(at.pb * at.neg_count, at.neg_count), at.neg_count)]
+    _, _, _, total_s, total_t, _ = query_terms(here)
+    grad_score = GRAD_SCALE * (
+        jnp.exp(score8) / total_s - jnp.exp(teacher8 / TEACHER_TEMP) / total_t
+    )
+    grad_unit = grad_score * gain
+    grad_resid = out_scale * (grad_unit - out_unit * lane_mean(grad_unit * out_unit))
+    resid_grad[...] = grad_resid
+    resid_cast = grad_resid.astype(bf16)
+    grad_context = stack_heads(mm(resid_cast, full_o[...])).astype(bf16)
+    context_blocks[...] = blocks_of(grad_context.astype(f32))
+    late_own[0:stacked, :] = grad_context
+
+    resid_parts = by_head(resid_cast.astype(f32))
+    for turn in range(turns):
+        packed = pack(resid_parts, turn).astype(bf16)
+        for index in range(model // HEAD_WIDTH):
+            resid_src[index * turns + turn] = tile(packed, index)
+    resid = Exchange(at, resid_src, resid_dst, resid_sems.at[0], resid_sems.at[1])
+    resid.start()
+
+    grad_probs = mm(context_blocks[...], value_cast[...], 1, 1)
+    spread = jnp.sum(attention_weights * grad_probs, axis=-1, keepdims=True)
+    logit_gradient = (attention_weights * (grad_probs - spread)).astype(bf16)
+    logit_grad[...] = logit_gradient
+
+    def key_back(pair, carry):
+        start = pl.multiple_of(pair * seq, seq)
+        rows = pl.ds(start, seq)
+        turned = mm(logit_grad[:, rows], query_blocks[...], 0, 0) * HEAD_WIDTH ** (-0.5)
+        for group in range(groups):
+            lanes = slice(group * HEAD_WIDTH, (group + 1) * HEAD_WIDTH)
+            part = turned[:, lanes]
+            unit = key_unit[rows, lanes]
+            back = part * cos_table[...] - pltpu.roll(part, HEAD_WIDTH // 2, 1) * sin_table[...]
+            back = key_scale[rows, lanes] * (back - unit * lane_mean(back * unit))
+            grad_k[rows, lanes] = back.astype(bf16)
+        return carry
+
+    lax.fori_loop(0, pairs, key_back, 0)
+
+    block_rows = model // at.pb_count
     copies = []
 
     def send(src, dst, send_sem, recv_sem, target):
@@ -499,10 +814,13 @@
         copies.append(copy)
 
     def arrive(block, recv_sem):
-        remote(block, block, loss_local, recv_sem, at.to_partner()).wait_recv()
+        remote(block, block, any_sem, recv_sem, at.to_partner()).wait_recv()
 
     for k in range(1, at.pb_count + 1):
         pb = at.pb_peer(k % at.pb_count)
+        lanes = pl.ds(pl.multiple_of(pb * block_rows, block_rows), block_rows)
+        product = mm(normed[:, lanes], grad_k[...], 0, 0)
+        partial[pb] = product.astype(bf16).reshape(at.line_count, 2, share, kv_width)
         send(
             partial.at[pb, :, at.partner],
             from_core.at[pb],
@@ -510,34 +828,63 @@
             core_recv.at[pb],
             at.to_partner(),
         )
-    gather.start()
-    local = pltpu.make_async_copy(loss_row, all_losses.at[at.pb], loss_local)
-    local.start()
-    for k in range(1, at.pb_count):
-        send(
-            loss_row, all_losses.at[at.pb], loss_send.at[k], loss_recv.at[at.pb], at.to_pb(at.pb_peer(k))
-        )
+
+    turned_q = diagonal_of(mm(logit_gradient, key_rot[...])) * HEAD_WIDTH ** (-0.5)
+    back_q = turned_q * cos_rows - pltpu.roll(turned_q, HEAD_WIDTH // 2, 1) * sin_rows
+    back_q = query_scale * (back_q - query_unit * lane_mean(back_q * query_unit))
+    grad_q_cast = back_q.astype(bf16)
+    late_own[stacked : 2 * stacked, :] = grad_q_cast
+
     for k in range(1, at.pb_count + 1):
         pb = at.pb_peer(k % at.pb_count)
         arrive(from_core.at[pb], core_recv.at[pb])
-        both = partial[pb, :, at.core].astype(jnp.float32) + from_core[pb].astype(jnp.float32)
-        paired[pb] = both.astype(jnp.bfloat16)
+        both = partial[pb, :, at.core].astype(f32) + from_core[pb].astype(f32)
+        paired[pb] = both.astype(bf16)
         if k < at.pb_count:
-            send(
-                paired.at[pb], from_pb.at[at.pb], pb_send.at[k], pb_recv.at[at.pb], at.to_pb(pb)
-            )
-    gather.middle()
-    gather.relay()
+            send(paired.at[pb], from_pb.at[at.pb], pb_send.at[k], pb_recv.at[at.pb], at.to_pb(pb))
+    gather_late.start()
+    gather_context.middle()
+    gather_context.relay()
+
+    back_last = mm(spread_heads(grad_q_cast.astype(f32)), full_q[...], 1, 1)
+    last_grad[...] = back_last + pltpu.roll(back_last, pairs, 0)
+
+    def value_back(pair, carry):
+        start = pl.multiple_of(pair * seq, seq)
+        rows = pl.ds(start, seq)
+        grad_v[rows, :] = mm(probs_ref[:, rows], context_blocks[...], 0, 0).astype(bf16)
+        return carry
+
+    lax.fori_loop(0, pairs, value_back, 0)
+
+    seq_row = lax.broadcasted_iota(jnp.int32, (seq, 1), 0)
+
+    def hidden_back(pair, carry):
+        rows = pl.ds(pl.multiple_of(pair * seq, seq), seq)
+        total = mm(grad_k[rows, :], full_k[...], 1, 1) + mm(grad_v[rows, :], full_v[...], 1, 1)
+        hit = seq_row == lengths[0, pair] - 1
+        total = total + jnp.where(hit, last_grad[pl.ds(pair, 1), :], 0.0)
+        scaled = total * norm_gain[...]
+        wide = x[rows, :].astype(f32)
+        inv = inv_wide[rows, 0:1]
+        mean = lane_mean(scaled * wide)
+        result = inv * scaled - wide * (inv * inv * inv * mean)
+        result = result + jnp.where(hit, resid_grad[pl.ds(pair, 1), :], 0.0)
+        grad_hidden[rows, :] = result.astype(bf16)
+        return carry
+
+    lax.fori_loop(0, pairs // 2, hidden_back, 0)
+
     for k in range(1, at.pb_count):
         pb = at.pb_peer(k)
         arrive(from_pb.at[pb], pb_recv.at[pb])
     for step in range(1, at.line_count + 1):
         line = at.line_peer(step % at.line_count)
-        total = paired[at.pb, line].astype(jnp.float32)
+        total = paired[at.pb, line].astype(f32)
         for k in range(1, at.pb_count):
-            total = total + from_pb[at.pb_peer(k), line].astype(jnp.float32)
+            total = total + from_pb[at.pb_peer(k), line].astype(f32)
         if step < at.line_count:
-            summed[line] = total.astype(jnp.bfloat16)
+            summed[line] = total.astype(bf16)
             send(
                 summed.at[line],
                 from_line.at[at.line],
@@ -545,57 +892,147 @@
                 line_recv.at[at.line],
                 at.to_line(line),
             )
+    gather_late.middle()
+    gather_late.relay()
+    gather_context.finish()
+
+    lax.fori_loop(pairs // 2, pairs, hidden_back, 0)
+
+    far_block = list_dst.at[pl.ds(0, at.count - at.neg_count)]
+    remote(far_block, far_block, list_sent, list_there, at.to_partner()).wait_recv()
+    loss = jnp.zeros((1, 1), f32)
+    for pb in range(at.pb_count):
+        block = list_dst[pb * at.neg_count : (pb + 1) * at.neg_count]
+        score, scaled, expo_t, sum_s, sum_t, total = query_terms(block)
+        loss = loss + total(expo_t / sum_t * (scaled - jnp.log(sum_t) - (score - jnp.log(sum_s))))
+    loss_out[...] = loss
+
+    gather_late.finish()
+    early.wait("wait_recv")
+    resid.wait("wait_recv")
+
+    def rows_of(full, start, group):
+        wide = full[...].astype(f32).reshape(at.count, -1, slots, HEAD_WIDTH)
+        return wide[:, start + group].reshape(at.count * slots, HEAD_WIDTH).astype(bf16)
+
+    pulled_rows = rows_of(early_dst, 0, 0)
+    last_rows = rows_of(early_dst, 1, 0)
+    resid_rows = rows_of(resid_dst, 0, 0)
+    for group in range(groups):
+        found = mm(pulled_rows, rows_of(late_full, 0, group), 0, 0)
+        lanes = slice(group * HEAD_WIDTH, (group + 1) * HEAD_WIDTH)
+        grad_value[:, lanes] = found[group * share : (group + 1) * share]
+        found = mm(last_rows, rows_of(late_full, groups, group), 0, 0)
+        for part in range(per_group):
+            head = per_group * group + part
+            grad_query[:, head * HEAD_WIDTH : (head + 1) * HEAD_WIDTH] = found[
+                part * share : (part + 1) * share
+            ]
+        found = mm(rows_of(context_full, 0, group), resid_rows, 0, 0)
+        for part in range(per_group):
+            head = per_group * group + part
+            moved = found if part == 0 else pltpu.roll(found, HEAD_WIDTH - part * share, 1)
+            grad_out[head * HEAD_WIDTH : (head + 1) * HEAD_WIDTH, :] = moved[:, :share]
+
     for step in range(1, at.line_count):
         line = at.line_peer(step)
         arrive(from_line.at[line], line_recv.at[line])
-        total = total + from_line[line].astype(jnp.float32)
-    reduced[...] = total
-    gather.finish()
-    local.wait()
+    final = paired[at.pb, at.line].astype(f32)
     for k in range(1, at.pb_count):
-        pb = at.pb_peer(k)
-        arrive(all_losses.at[pb], loss_recv.at[pb])
+        final = final + from_pb[at.pb_peer(k), at.line].astype(f32)
+    for step in range(1, at.line_count):
+        final = final + from_line[at.line_peer(step)].astype(f32)
+    grad_key[...] = final
+
+    for gather in gathers:
+        gather.drain()
     for copy in copies:
         copy.wait_send()
-
-
-def reduce_gradients(grad_kv, last_rows, loss_row, pb_count, neg_count):
+    early.wait("wait_send")
+    resid.wait("wait_send")
+    sent_block = list_dst.at[pl.ds(0, at.count - 1)]
+    remote(sent_block, sent_block, list_sent, list_here, at.to_partner()).wait_send()
+
+
+def run_step(operands, sizes, pb_count, neg_count):
+    pairs, seq, groups, share = sizes
+    x, own_q, own_k = operands[0], operands[8], operands[9]
+    model, width, kv_width = x.shape[1], own_q.shape[1], own_k.shape[1]
+    rows = pairs * seq
+    count = pb_count * neg_count
     line_count = neg_count // 2
-    share = grad_kv.shape[0] // (pb_count * neg_count)
-    width = grad_kv.shape[1]
-    partial = grad_kv.reshape(pb_count, line_count, 2, share, width)
-    block = (pb_count, line_count, share, width)
+    slots = width // kv_width * pairs
+    stacked = groups * slots
+    bf16, f32 = jnp.bfloat16, jnp.float32
+    block = (pb_count, line_count, share, kv_width)
     dma = pltpu.SemaphoreType.DMA
+    vmem = pltpu.VMEM
+    smem_spec = pl.BlockSpec(memory_space=pltpu.SMEM)
     return pl.pallas_call(
-        reduce_kernel,
+        functools.partial(step_kernel, sizes),
         out_shape=(
-            jax.ShapeDtypeStruct((share, width), jnp.float32),
-            jax.ShapeDtypeStruct((last_rows.shape[0] * pb_count * neg_count, last_rows.shape[1]), last_rows.dtype),
-            jax.ShapeDtypeStruct((pb_count,) + loss_row.shape, loss_row.dtype),
+            jax.ShapeDtypeStruct((1, pairs), f32),
+            jax.ShapeDtypeStruct((1, 1), f32),
+            jax.ShapeDtypeStruct((rows, model), bf16),
+            jax.ShapeDtypeStruct((share, width), f32),
+            jax.ShapeDtypeStruct((share, kv_width), f32),
+            jax.ShapeDtypeStruct((share, kv_width), f32),
+            jax.ShapeDtypeStruct((width, share), f32),
         ),
-        in_specs=[VMEM_SPEC] * 3,
-        out_specs=(VMEM_SPEC,) * 3,
+        in_specs=[VMEM_SPEC, smem_spec, smem_spec] + [VMEM_SPEC] * 9,
+        out_specs=(VMEM_SPEC,) * 7,
         scratch_shapes=[
-            pltpu.VMEM(block, jnp.bfloat16),
-            pltpu.VMEM(block, jnp.bfloat16),
-            pltpu.VMEM(block, jnp.bfloat16),
-            pltpu.VMEM(block[1:], jnp.bfloat16),
-            pltpu.VMEM(block[1:], jnp.bfloat16),
+            vmem((share, width), bf16),
+            vmem((model, width), bf16),
+            vmem((model, kv_width), bf16),
+            vmem((model, kv_width), bf16),
+            vmem((model, width), bf16),
+            vmem((rows, model), bf16),
+            vmem((rows, HEAD_WIDTH), f32),
+            vmem((rows, kv_width), f32),
+            vmem((rows, kv_width), f32),
+            vmem((rows, kv_width), bf16),
+            vmem((rows, kv_width), bf16),
+            vmem((rows, kv_width), bf16),
+            vmem((rows, kv_width), bf16),
+            vmem((stacked, rows), bf16),
+            vmem((stacked, rows), bf16),
+            vmem((stacked, kv_width), bf16),
+            vmem((stacked, kv_width), bf16),
+            vmem((slots, model), f32),
+            vmem((slots, model), f32),
+            vmem((stacked, HEAD_WIDTH), bf16),
+            vmem((stacked * count, HEAD_WIDTH), bf16),
+            vmem((2 * stacked, HEAD_WIDTH), bf16),
+            vmem((2 * stacked * count, HEAD_WIDTH), bf16),
+            vmem((count, 2 * slots, HEAD_WIDTH), bf16),
+            vmem((count, 2 * slots, HEAD_WIDTH), bf16),
+            vmem((count, slots, HEAD_WIDTH), bf16),
+            vmem((count, slots, HEAD_WIDTH), bf16),
+            vmem((slots, HEAD_WIDTH), f32),
+            vmem((count, slots, HEAD_WIDTH), f32),
+            vmem((pb_count, line_count, 2, share, kv_width), bf16),
+            vmem(block, bf16),
+            vmem(block, bf16),
+            vmem(block, bf16),
+            vmem(block[1:], bf16),
+            vmem(block[1:], bf16),
+            dma((2,)),
+            dma((2,)),
+            dma((3,)),
             dma((pb_count,)),
             dma((pb_count,)),
             dma((pb_count,)),
             dma((pb_count,)),
             dma((line_count,)),
             dma((line_count,)),
-            dma((pb_count,)),
-            dma((pb_count,)),
             dma,
         ]
-        + gather_sems(pb_count, neg_count),
+        + gather_sems(pb_count, neg_count) * 6,
         compiler_params=pltpu.CompilerParams(
-            collective_id=2, has_side_effects=True, vmem_limit_bytes=40 * 2**20
+            collective_id=0, has_side_effects=True, vmem_limit_bytes=60 * 2**20
         ),
-    )(partial, last_rows, loss_row)
+    )(*operands)
 
 
 def shards(
@@ -613,38 +1050,63 @@
     both = ("pb", "neg")
     width = query_weight.shape[1]
     kv_width = key_matrix.shape[1]
-    shares = (query_weight, key_matrix, value_matrix, out_weight.T)
+    share, out_share = query_weight.shape[0], out_weight.shape[1]
     pb_count, neg_count = lax.axis_size("pb"), lax.axis_size("neg")
-    even = all(w.shape[0] % 16 == 0 and w.shape[1] % (2 * HEAD_WIDTH) == 0 for w in shares)
-    own_kernels = even and pb_count == 4 and neg_count % 2 == 0
+    pair_count, seq_len, model_width = hidden.shape[1:]
+    group_count = kv_width // HEAD_WIDTH
+    own_kernels = (
+        pb_count == 4
+        and neg_count % 2 == 0
+        and share == out_share
+        and share % 32 == 0
+        and model_width == share * pb_count * neg_count
+        and width == 2 * kv_width
+        and pair_count * 2 == 8
+        and seq_len == HEAD_WIDTH
+        and share * group_count == HEAD_WIDTH
+    )
     if own_kernels:
-        full_query, full_key, full_value, full_out_t = gather_weights(shares, pb_count, neg_count)
-    else:
-        packed = jnp.concatenate(shares, axis=1)
-        everything = lax.all_gather(packed, both, axis=0, tiled=True)
-        full_query = everything[:, :width]
-        full_key = everything[:, width : width + kv_width]
-        full_value = everything[:, width + kv_width : width + 2 * kv_width]
-        full_out_t = everything[:, width + 2 * kv_width :]
+        cos_table, sin_table = signed_tables(seq_len, HEAD_WIDTH)
+        scores, loss, grad_rows, grad_query, grad_key, grad_value, grad_out = run_step(
+            (
+                hidden.reshape(pair_count * seq_len, model_width),
+                lengths,
+                teacher,
+                norm_gain[None],
+                final_gain[None],
+                score_vector[None],
+                cos_table,
+                sin_table,
+                query_weight,
+                key_matrix,
+                value_matrix,
+                out_weight,
+            ),
+            (pair_count, seq_len, group_count, share),
+            pb_count,
+            neg_count,
+        )
+        return (
+            scores,
+            loss.reshape(()),
+            grad_rows.reshape(hidden.shape),
+            grad_query,
+            grad_key,
+            grad_value,
+            grad_out,
+        )
+    packed = jnp.concatenate([query_weight, key_matrix, value_matrix, out_weight.T], axis=1)
+    everything = lax.all_gather(packed, both, axis=0, tiled=True)
+    full_query = everything[:, :width]
+    full_key = everything[:, width : width + kv_width]
+    full_value = everything[:, width + kv_width : width + 2 * kv_width]
+    full_out_t = everything[:, width + 2 * kv_width :]
+    weights = (full_query, full_key, full_value, full_out_t.T)
     scores_here, stored = forward_pairs(
-        hidden[0],
-        lengths[0],
-        norm_gain,
-        final_gain,
-        score_vector,
-        full_query,
-        full_key,
-        full_value,
-        full_out_t.T,
-    )
-    pair_count = scores_here.shape[0]
-    row = lax.axis_index("pb")
+        hidden[0], lengths[0], norm_gain, final_gain, score_vector, *weights
+    )
     listing = jnp.concatenate([scores_here, teacher[0]])[None]
-    if own_kernels:
-        lanes = jnp.pad(listing, ((0, 0), (0, HEAD_WIDTH - 2 * pair_count)))
-        listed = exchange_listing(lanes, neg_count)[:, 0, : 2 * pair_count]
-    else:
-        listed = lax.all_gather(listing, "neg", axis=0, tiled=True)
+    listed = lax.all_gather(listing, "neg", axis=0, tiled=True)
     all_scores = listed[:, :pair_count]
     all_scaled = listed[:, pair_count:] / TEACHER_TEMP
     my_total_s = jnp.sum(jnp.exp(all_scores))
@@ -659,34 +1121,14 @@
     prob_t = jnp.exp(teacher[0] / TEACHER_TEMP) / my_total_t
     grad_score = GRAD_SCALE * (prob_s - prob_t)
     grad_input, last_rows, grad_kv = backward_pairs(
-        stored,
-        grad_score,
-        norm_gain,
-        final_gain,
-        score_vector,
-        full_query,
-        full_key,
-        full_value,
-        full_out_t.T,
+        stored, grad_score, norm_gain, final_gain, score_vector, *weights
     )
     grad_kv = grad_kv.astype(jnp.bfloat16)
-    if own_kernels:
-        spaced = jnp.pad(last_rows.reshape(pair_count * 4, -1), ((0, -pair_count * 4 % 16), (0, 0)))
-        reduced, rows, losses = reduce_gradients(
-            grad_kv, spaced, jnp.full((1, HEAD_WIDTH), loss_here), pb_count, neg_count
-        )
-        rows = rows.reshape(-1, spaced.shape[0], spaced.shape[1])[:, : pair_count * 4]
-        rows = rows.reshape(pb_count * neg_count * pair_count, -1)
-        loss_value = jnp.sum(losses[:, 0, 0])
-    else:
-        reduced = lax.psum_scatter(grad_kv, both, scatter_dimension=0, tiled=True)
-        reduced = reduced.astype(jnp.float32)
-        rows = lax.all_gather(last_rows, both, axis=0, tiled=True)
-        loss_value = lax.psum(loss_here, "pb")
-    index = row * lax.axis_size("neg") + lax.axis_index("neg")
-    share = query_weight.shape[0]
-    model_width = share * lax.axis_size("pb") * lax.axis_size("neg")
-    out_share = out_weight.shape[1]
+    reduced = lax.psum_scatter(grad_kv, both, scatter_dimension=0, tiled=True)
+    reduced = reduced.astype(jnp.float32)
+    rows = lax.all_gather(last_rows, both, axis=0, tiled=True)
+    loss_value = lax.psum(loss_here, "pb")
+    index = lax.axis_index("pb") * neg_count + lax.axis_index("neg")
     normed_cols = lax.dynamic_slice_in_dim(rows, index * share, share, axis=1)
     resid_cols = lax.dynamic_slice_in_dim(rows, model_width + index * out_share, out_share, axis=1)
     rest = 2 * model_width

time: 144 us -> 88.6 us (0.62)
  matrix products: 26.2 us -> 0 us
  other arithmetic: 20 us -> 0 us
  local copies, waits for them, and re-layouts: 17.8 us -> 8.72 us
    dot_general x19 -> x0, matrix products: 26.2 us -> none  [the longest x1 3.11 us: forward_pairs(): jnp.dot(flat_rows, value_matrix, preferred_element_type=jnp.float32)]
    convert_element_type x10 -> x0, other arithmetic: 6.86 us -> none  [the longest x1 2.47 us: backward_pairs(): return (grad_input.astype(jnp.bfloat16), last_rows, grad_kv)]
    reduce_sum x8 -> x0, other arithmetic: 6.48 us -> none  [the longest x1 2.08 us: shards(): jnp.sum(expo_t / my_total_t * (all_scaled - jnp.log(my_total_t) - (all_sc...]
    dot_general x3 -> x0, local copies, waits for them, and re-layouts: 6.17 us -> none  [the longest x1 2.6 us: forward_pairs(): jnp.dot(normed_last, query_weight, preferred_element_type=jnp.float32)]
    unnamed x65 -> x15, local copies, waits for them, and re-layouts: 3.94 us -> 8.72 us
    convert_element_type x3 -> x0, local copies, waits for them, and re-layouts: 3.32 us -> none  [the longest x1 2.09 us: backward_pairs(): grad_kproj.reshape(pair_count * seq_len, group_count * HEAD_WIDTH)]
    mul x6 -> x0, other arithmetic: 2.47 us -> none  [the longest x1 1.3 us: shards(): grad_score = GRAD_SCALE * (prob_s - prob_t)]
    gather x2 -> x0, local copies, waits for them, and re-layouts: 1.79 us -> none  [the longest x1 1.18 us: forward_pairs(): jnp.take_along_axis(inputs_wide, last_index[:, None, None], axis=1)[:, 0]]
where the time goes in v1:
time: 88.6 us; the launch traced here: 88.2 us
  Pallas kernels  77.1 us (87%)
  local copies, waits for them, and re-layouts  8.72 us (10%)
  between operations  2.41 us (3%)
    pallas_call x1, Pallas kernels, run_step(): pl.pallas_call(functools.partial(step_kernel, sizes), out_shape=(jax.Shap...  77.1 us
    unnamed x15, local copies, waits for them, and re-layouts  8.72 us

profile of v1, /device:TPU:0, one launch (start us, length us, event | category | flops | bytes accessed | tf_op | source)
XLA Modules:
  0.0 88.2 jit_solution(3114996645737095065)
XLA Ops:
  0.6 1.7 %copy.19.own_out = bf16[1024,32]{1,0:T(8,128)(2,1)} copy(bf16[1024,32]{0,1:T(8,128)(2,1)} %param.21) | data formatting | bytes 131072 | tf_op args[9]
  2.3 77.1 %shard_map.171 = (f32[1,4]{1,0:T(1,128)}, f32[1,1]{1,0:T(1,128)}, bf16[512,1024]{1,0:T(8,128)(2,1)}, f32[32,1024]{1,0:T(8,128)}, f32[32,512]{1,0:T(8,128)}, /*index=5*/f32[32,512]{1,0:T(8,128)}, f32[1024,32]{1,0:T(8,128)}) custom-call(bf16[512,1024]{1,0:T(8,128)(2,1)} %bitcast.6, s32[1,4]{1,0:T(1,128)} %lengths.1, f32[1,4]{1,0:T(1,128)} %teacher.1, ...), custom_call_target="tpu_custom_call" | custom-call | tf_op jit(solution)/shard_map/pallas_call | solution.py:971
  79.4 0.0 copy-start.3
  79.4 1.9 %copy.20 = f32[1024,32]{0,1:T(8,128)} copy(f32[1024,32]{1,0:T(8,128)} %get-tuple-element.27) | data formatting | bytes 262144
  81.3 0.0 copy-done.3
  81.3 0.5 copy.27
  82.4 0.0 copy-start
  82.4 2.3 %copy.29 = bf16[1,4,128,1024]{3,2,1,0:T(8,128)(2,1)} copy(bf16[1,4,128,1024]{3,2,1,0:T(8,128)(2,1)} %bitcast.7) | data formatting | bytes 2097152
  84.7 0.0 copy-done
  84.7 0.0 copy-start.2
  84.7 0.7 copy.30
  85.4 0.2 copy-done.2
  85.6 0.0 copy-start.1
  85.6 0.6 copy.31
  86.2 0.2 copy-done.1
  86.5 0.6 copy.32
Async XLA Ops:
  79.4 1.9 %copy-start.3 = (f32[1,4]{1,0:T(1,128)S(1)}, f32[1,4]{1,0:T(1,128)}, u32[]{:S(2)}) copy-start(f32[1,4]{1,0:T(1,128)} %get-tuple-element.35) | copy-start | bytes 52
  82.4 2.3 %copy-start = (f32[32,1024]{1,0:T(8,128)S(1)}, f32[32,1024]{1,0:T(8,128)}, u32[]{:S(2)}) copy-start(f32[32,1024]{1,0:T(8,128)} %get-tuple-element.38) | copy-start | bytes 393220
  84.7 0.9 copy-start.2
  85.6 0.9 copy-start.1

commit v2 on v1

--- a/solution.py
+++ b/solution.py
@@ -429,16 +429,11 @@
 
     def start(self):
         at = self.at
-
-        def one(step, carry):
-            peer = lax.rem(at.me + step, at.count)
-            target = (peer // at.neg_count, lax.rem(peer, at.neg_count))
+        for pb, neg in at.others:
+            peer = pb * at.neg_count + neg
             remote(
-                self.src.at[peer], self.dst.at[at.me], self.send_sem, self.recv_sem, target
+                self.src.at[peer], self.dst.at[at.me], self.send_sem, self.recv_sem, (pb, neg)
             ).start()
-            return carry
-
-        lax.fori_loop(1, at.count, one, 0)
         self.dst[at.me] = self.src[at.me]
 
     def wait(self, sem_of):
@@ -449,9 +444,26 @@
 
 def step_kernel(
     sizes,
-    x,
+    hidden,
     lengths,
     teacher,
+    norm_gain_in,
+    final_gain_in,
+    score_vector_in,
+    cos_table_in,
+    sin_table_in,
+    own_q_in,
+    own_k_in,
+    own_v_in,
+    own_o_in,
+    scores_out,
+    loss_out,
+    grad_hidden,
+    grad_query,
+    grad_key,
+    grad_value,
+    grad_out,
+    x,
     norm_gain,
     final_gain,
     score_vector,
@@ -460,14 +472,6 @@
     own_q,
     own_k,
     own_v,
-    own_out,
-    scores_out,
-    loss_out,
-    grad_hidden,
-    grad_query,
-    grad_key,
-    grad_value,
-    grad_out,
     own_o,
     full_q,
     full_k,
@@ -513,6 +517,7 @@
     line_send,
     line_recv,
     any_sem,
+    load_sems,
     *gather_sem_refs,
 ):
     pairs, seq, groups, share = sizes
@@ -520,6 +525,15 @@
     at = Place()
     at.count = at.pb_count * at.neg_count
     at.me = at.slot(at.pb, at.line, at.core)
+    neg = lax.axis_index("neg")
+    pb_all = [at.pb] + [at.pb_peer(k) for k in range(1, at.pb_count)]
+    neg_all = [neg] + [lax.rem(neg + k, at.neg_count) for k in range(1, at.neg_count)]
+    at.others = [
+        (pb, peer)
+        for i, pb in enumerate(pb_all)
+        for j, peer in enumerate(neg_all)
+        if i + j > 0
+    ]
     model = x.shape[1]
     rows_all = pairs * seq
     per_group = own_q.shape[1] // own_k.shape[1]
@@ -529,13 +543,30 @@
 
     barrier = pltpu.get_barrier_semaphore()
 
-    def greet(step, carry):
-        peer = lax.rem(at.me + step, at.count)
-        target = (peer // at.neg_count, lax.rem(peer, at.neg_count))
+    for target in at.others:
         pl.semaphore_signal(barrier, inc=1, device_id=target, device_id_type=MESH_ID)
-        return carry
-
-    lax.fori_loop(1, at.count, greet, 0)
+    loads = []
+    moves = (
+        (own_k_in, own_k),
+        (own_v_in, own_v),
+        (own_q_in, own_q),
+        (own_o_in, own_o),
+        (norm_gain_in, norm_gain),
+        (final_gain_in, final_gain),
+        (score_vector_in, score_vector),
+        (cos_table_in, cos_table),
+        (sin_table_in, sin_table),
+    )
+    small_loads = []
+    for place_of, (source, target) in enumerate(moves):
+        load = pltpu.make_async_copy(source, target, load_sems.at[pairs + place_of])
+        load.start()
+        small_loads.append(load)
+    for pair in range(pairs):
+        rows = pl.ds(pair * seq, seq)
+        load = pltpu.make_async_copy(hidden.at[rows], x.at[rows], load_sems.at[pair])
+        load.start()
+        loads.append(load)
 
     each = len(gather_sem_refs) // 6
     gathers = []
@@ -553,17 +584,6 @@
         gathers.append(Gather(at, own, full, sems))
     gather_k, gather_v, gather_q, gather_o, gather_context, gather_late = gathers
 
-    diagonal = lax.broadcasted_iota(jnp.int32, (share, share), 0) == lax.broadcasted_iota(
-        jnp.int32, (share, share), 1
-    )
-    own_o[...] = mm(diagonal.astype(f32).astype(bf16), own_out[...], 1, 1).astype(bf16)
-
-    pl.semaphore_wait(barrier, at.count - 1)
-    gather_k.start()
-    gather_v.start()
-    gather_q.start()
-    gather_o.start()
-
     def norm_pair(pair, carry):
         rows = pl.ds(pl.multiple_of(pair * seq, seq), seq)
         wide = x[rows, :].astype(f32)
@@ -572,7 +592,11 @@
         normed[rows, :] = (wide * inv * norm_gain[...]).astype(bf16)
         return carry
 
-    lax.fori_loop(0, pairs, norm_pair, 0)
+    for load in small_loads:
+        load.wait()
+    for pair in range(pairs):
+        loads[pair].wait()
+        norm_pair(pair, 0)
 
     row8 = lax.broadcasted_iota(jnp.int32, (slots, 1), 0)
     pair8 = lax.rem(row8, pairs)
@@ -589,10 +613,6 @@
     visible = jnp.concatenate([visible8.astype(f32)] * groups, axis=0) > 0.5
     position8 = (lax.broadcasted_iota(jnp.int32, (slots, seq), 1) == last8).astype(f32)
 
-    gather_k.middle()
-    gather_v.middle()
-    gather_k.relay()
-
     x_last = mm(onehot8, x[...])
     normed_last = mm(onehot8, normed[...]).astype(bf16)
     cos8 = mm(position8, cos_table[...], precision=lax.Precision.HIGHEST)
@@ -600,6 +620,14 @@
     cos_rows = jnp.concatenate([cos8] * groups, axis=0)
     sin_rows = jnp.concatenate([sin8] * groups, axis=0)
 
+    pl.semaphore_wait(barrier, at.count - 1)
+    gather_k.start()
+    gather_v.start()
+    gather_q.start()
+    gather_o.start()
+    gather_k.middle()
+    gather_v.middle()
+    gather_k.relay()
     gather_q.middle()
     gather_v.relay()
     gather_k.finish()
@@ -685,6 +713,7 @@
     context = diagonal_of(mm(probs, value_cast[...]))
     context_own[...] = context.astype(bf16)
     context_wide = spread_heads(context)
+    gather_context.start()
 
     lane_block = lax.rem(
         lax.broadcasted_iota(jnp.int32, (slots, model), 1) // share, HEAD_WIDTH // share
@@ -711,6 +740,9 @@
         for index in range(model // HEAD_WIDTH):
             early_src[index * turns + turn] = tile(both, index)
 
+    early = Exchange(at, early_src, early_dst, early_sems.at[0], early_sems.at[1])
+    early.start()
+
     gather_o.finish()
     attended = mm(context_wide, full_o[...], 1, 1)
     attended = attended + pltpu.roll(attended, pairs, 0)
@@ -721,51 +753,42 @@
     score8 = jnp.sum(out_unit * gain, axis=-1, keepdims=True)
 
     lane8 = lax.broadcasted_iota(jnp.int32, (slots, HEAD_WIDTH), 1)
-    listing = jnp.where(lane8 == 0, score8, jnp.where(lane8 == 1, teacher8, 0.0))
+    row_lane = lax.broadcasted_iota(jnp.int32, (slots, HEAD_WIDTH), 0)
+
+    def as_row(column):
+        return jnp.sum(jnp.where(row_lane == lane8, column, 0.0), axis=0, keepdims=True)
+
+    score_row = as_row(score8)
+    lane1 = lax.broadcasted_iota(jnp.int32, (1, HEAD_WIDTH), 1)
+    listing = jnp.where(lane1 < pairs, score_row, as_row(teacher8))
     list_src[...] = listing
-    me_tile = list_dst.at[at.me]
+    me_row = list_dst.at[at.me]
     list_here, list_there, list_sent = list_sems.at[0], list_sems.at[1], list_sems.at[2]
-    neg = lax.axis_index("neg")
-
-    def list_near(step, carry):
-        peer = lax.rem(neg + step, at.neg_count)
-        remote(list_src, me_tile, list_sent, list_here, (at.pb, peer)).start()
-        return carry
-
-    def list_far(step, carry):
-        peer = lax.rem(neg + step, at.neg_count)
-        for k in range(1, at.pb_count):
-            remote(list_src, me_tile, list_sent, list_there, (at.pb_peer(k), peer)).start()
-        return carry
-
-    lax.fori_loop(1, at.neg_count, list_near, 0)
-    lax.fori_loop(0, at.neg_count, list_far, 0)
+    for place_of, target in enumerate(at.others):
+        arrived = list_here if place_of < at.neg_count - 1 else list_there
+        remote(list_src, me_row, list_sent, arrived, target).start()
     list_dst[at.me] = listing
-    early = Exchange(at, early_src, early_dst, early_sems.at[0], early_sems.at[1])
-    gather_context.start()
-    early.start()
-
-    row_lane = lax.broadcasted_iota(jnp.int32, (slots, HEAD_WIDTH), 0)
-    score_row = jnp.sum(jnp.where(row_lane == lane8, score8, 0.0), axis=0, keepdims=True)
     scores_out[...] = score_row[:, :pairs]
+    gather_context.middle()
+    gather_context.relay()
 
     near_block = list_dst.at[pl.ds(0, at.neg_count - 1)]
     remote(near_block, near_block, list_sent, list_here, at.to_partner()).wait_recv()
 
-    real3 = lax.broadcasted_iota(jnp.int32, (at.neg_count, slots, 1), 1) < pairs
-    lane3 = lax.broadcasted_iota(jnp.int32, (at.neg_count, slots, HEAD_WIDTH), 2)
-
-    def query_terms(block):
-        score = jnp.sum(jnp.where(lane3 == 0, block, 0.0), axis=-1, keepdims=True)
-        scaled = jnp.sum(jnp.where(lane3 == 1, block, 0.0), axis=-1, keepdims=True) / TEACHER_TEMP
-        total = lambda array: jnp.sum(
-            jnp.sum(jnp.where(real3, array, 0.0), axis=0), axis=0, keepdims=True
-        )
-        expo_t = jnp.exp(scaled)
-        return score, scaled, expo_t, total(jnp.exp(score)), total(expo_t), total
-
-    here = list_dst[pl.ds(pl.multiple_of(at.pb * at.neg_count, at.neg_count), at.neg_count)]
-    _, _, _, total_s, total_t, _ = query_terms(here)
+    def total(array):
+        return jnp.sum(jnp.sum(array, axis=1, keepdims=True), axis=0, keepdims=True)
+
+    def query_terms(first):
+        block = list_dst[pl.ds(first, at.neg_count)].reshape(at.neg_count, HEAD_WIDTH)
+        real = lax.broadcasted_iota(jnp.int32, block.shape, 1) < pairs
+        score = jnp.where(real, block, 0.0)
+        scaled = pltpu.roll(block, HEAD_WIDTH - pairs, 1)
+        scaled = jnp.where(real, scaled, 0.0) / TEACHER_TEMP
+        expo_t = jnp.where(real, jnp.exp(scaled), 0.0)
+        total_s = total(jnp.where(real, jnp.exp(score), 0.0))
+        return score, scaled, expo_t, total_s, total(expo_t)
+
+    _, _, _, total_s, total_t = query_terms(pl.multiple_of(at.pb * at.neg_count, at.neg_count))
     grad_score = GRAD_SCALE * (
         jnp.exp(score8) / total_s - jnp.exp(teacher8 / TEACHER_TEMP) / total_t
     )
@@ -777,18 +800,17 @@
     context_blocks[...] = blocks_of(grad_context.astype(f32))
     late_own[0:stacked, :] = grad_context
 
-    resid_parts = by_head(resid_cast.astype(f32))
-    for turn in range(turns):
-        packed = pack(resid_parts, turn).astype(bf16)
-        for index in range(model // HEAD_WIDTH):
-            resid_src[index * turns + turn] = tile(packed, index)
-    resid = Exchange(at, resid_src, resid_dst, resid_sems.at[0], resid_sems.at[1])
-    resid.start()
-
     grad_probs = mm(context_blocks[...], value_cast[...], 1, 1)
     spread = jnp.sum(attention_weights * grad_probs, axis=-1, keepdims=True)
     logit_gradient = (attention_weights * (grad_probs - spread)).astype(bf16)
     logit_grad[...] = logit_gradient
+
+    turned_q = diagonal_of(mm(logit_gradient, key_rot[...])) * HEAD_WIDTH ** (-0.5)
+    back_q = turned_q * cos_rows - pltpu.roll(turned_q, HEAD_WIDTH // 2, 1) * sin_rows
+    back_q = query_scale * (back_q - query_unit * lane_mean(back_q * query_unit))
+    grad_q_cast = back_q.astype(bf16)
+    late_own[stacked : 2 * stacked, :] = grad_q_cast
+    gather_late.start()
 
     def key_back(pair, carry):
         start = pl.multiple_of(pair * seq, seq)
@@ -829,22 +851,34 @@
             at.to_partner(),
         )
 
-    turned_q = diagonal_of(mm(logit_gradient, key_rot[...])) * HEAD_WIDTH ** (-0.5)
-    back_q = turned_q * cos_rows - pltpu.roll(turned_q, HEAD_WIDTH // 2, 1) * sin_rows
-    back_q = query_scale * (back_q - query_unit * lane_mean(back_q * query_unit))
-    grad_q_cast = back_q.astype(bf16)
-    late_own[stacked : 2 * stacked, :] = grad_q_cast
-
     for k in range(1, at.pb_count + 1):
         pb = at.pb_peer(k % at.pb_count)
         arrive(from_core.at[pb], core_recv.at[pb])
         both = partial[pb, :, at.core].astype(f32) + from_core[pb].astype(f32)
         paired[pb] = both.astype(bf16)
-        if k < at.pb_count:
-            send(paired.at[pb], from_pb.at[at.pb], pb_send.at[k], pb_recv.at[at.pb], at.to_pb(pb))
-    gather_late.start()
-    gather_context.middle()
-    gather_context.relay()
+    for step in range(1, at.line_count + 1):
+        line = at.line_peer(step % at.line_count)
+        for k in range(1, at.pb_count):
+            pb = at.pb_peer(k)
+            send(
+                paired.at[pb, line],
+                from_pb.at[at.pb, line],
+                pb_send.at[k, line],
+                pb_recv.at[at.pb, line],
+                at.to_pb(pb),
+            )
+
+    resid_parts = by_head(resid_cast.astype(f32))
+    for turn in range(turns):
+        packed = pack(resid_parts, turn).astype(bf16)
+        for index in range(model // HEAD_WIDTH):
+            resid_src[index * turns + turn] = tile(packed, index)
+    resid = Exchange(at, resid_src, resid_dst, resid_sems.at[0], resid_sems.at[1])
+    resid.start()
+
+    gather_late.middle()
+    gather_late.relay()
+    gather_context.finish()
 
     back_last = mm(spread_heads(grad_q_cast.astype(f32)), full_q[...], 1, 1)
     last_grad[...] = back_last + pltpu.roll(back_last, pairs, 0)
@@ -873,16 +907,13 @@
         grad_hidden[rows, :] = result.astype(bf16)
         return carry
 
-    lax.fori_loop(0, pairs // 2, hidden_back, 0)
-
-    for k in range(1, at.pb_count):
-        pb = at.pb_peer(k)
-        arrive(from_pb.at[pb], pb_recv.at[pb])
-    for step in range(1, at.line_count + 1):
+    def add_line(step):
         line = at.line_peer(step % at.line_count)
         total = paired[at.pb, line].astype(f32)
         for k in range(1, at.pb_count):
-            total = total + from_pb[at.pb_peer(k), line].astype(f32)
+            pb = at.pb_peer(k)
+            arrive(from_pb.at[pb, line], pb_recv.at[pb, line])
+            total = total + from_pb[pb, line].astype(f32)
         if step < at.line_count:
             summed[line] = total.astype(bf16)
             send(
@@ -892,18 +923,23 @@
                 line_recv.at[at.line],
                 at.to_line(line),
             )
-    gather_late.middle()
-    gather_late.relay()
-    gather_context.finish()
-
-    lax.fori_loop(pairs // 2, pairs, hidden_back, 0)
+        return total
+
+    hidden_back(0, 0)
+    add_line(1)
+    hidden_back(1, 0)
+    add_line(2)
+    hidden_back(2, 0)
+    for step in range(3, at.line_count + 1):
+        own_sum = add_line(step)
+    for pair in range(3, pairs):
+        hidden_back(pair, 0)
 
     far_block = list_dst.at[pl.ds(0, at.count - at.neg_count)]
     remote(far_block, far_block, list_sent, list_there, at.to_partner()).wait_recv()
     loss = jnp.zeros((1, 1), f32)
     for pb in range(at.pb_count):
-        block = list_dst[pb * at.neg_count : (pb + 1) * at.neg_count]
-        score, scaled, expo_t, sum_s, sum_t, total = query_terms(block)
+        score, scaled, expo_t, sum_s, sum_t = query_terms(pb * at.neg_count)
         loss = loss + total(expo_t / sum_t * (scaled - jnp.log(sum_t) - (score - jnp.log(sum_s))))
     loss_out[...] = loss
 
@@ -928,20 +964,18 @@
             grad_query[:, head * HEAD_WIDTH : (head + 1) * HEAD_WIDTH] = found[
                 part * share : (part + 1) * share
             ]
-        found = mm(rows_of(context_full, 0, group), resid_rows, 0, 0)
+        found = mm(resid_rows, rows_of(context_full, 0, group), 0, 0)
         for part in range(per_group):
             head = per_group * group + part
-            moved = found if part == 0 else pltpu.roll(found, HEAD_WIDTH - part * share, 1)
-            grad_out[head * HEAD_WIDTH : (head + 1) * HEAD_WIDTH, :] = moved[:, :share]
-
+            grad_out[:, head * HEAD_WIDTH : (head + 1) * HEAD_WIDTH] = found[
+                part * share : (part + 1) * share
+            ]
+
+    final = own_sum
     for step in range(1, at.line_count):
         line = at.line_peer(step)
         arrive(from_line.at[line], line_recv.at[line])
-    final = paired[at.pb, at.line].astype(f32)
-    for k in range(1, at.pb_count):
-        final = final + from_pb[at.pb_peer(k), at.line].astype(f32)
-    for step in range(1, at.line_count):
-        final = final + from_line[at.line_peer(step)].astype(f32)
+        final = final + from_line[line].astype(f32)
     grad_key[...] = final
 
     for gather in gathers:
@@ -952,6 +986,31 @@
     resid.wait("wait_send")
     sent_block = list_dst.at[pl.ds(0, at.count - 1)]
     remote(sent_block, sent_block, list_sent, list_here, at.to_partner()).wait_send()
+
+
+def write_kernel(count, *refs):
+    sources, targets, sems = refs[:count], refs[count : 2 * count], refs[2 * count]
+    copies = [
+        pltpu.make_async_copy(sources[i], targets[i], sems.at[i]) for i in range(2, count)
+    ]
+    for copy in copies:
+        copy.start()
+    for i in range(2):
+        targets[i][...] = sources[i][...]
+    for copy in copies:
+        copy.wait()
+
+
+def write_outputs(arrays):
+    count = len(arrays)
+    return pl.pallas_call(
+        functools.partial(write_kernel, count),
+        out_shape=tuple(jax.ShapeDtypeStruct(a.shape, a.dtype) for a in arrays),
+        in_specs=[VMEM_SPEC] * count,
+        out_specs=(VMEM_SPEC,) * 2 + (pl.BlockSpec(memory_space=pl.ANY),) * (count - 2),
+        scratch_shapes=[pltpu.SemaphoreType.DMA((count,))],
+        compiler_params=pltpu.CompilerParams(vmem_limit_bytes=4 * 2**20),
+    )(*arrays)
 
 
 def run_step(operands, sizes, pb_count, neg_count):
@@ -968,21 +1027,25 @@
     dma = pltpu.SemaphoreType.DMA
     vmem = pltpu.VMEM
     smem_spec = pl.BlockSpec(memory_space=pltpu.SMEM)
+    hbm_spec = pl.BlockSpec(memory_space=pltpu.HBM)
     return pl.pallas_call(
         functools.partial(step_kernel, sizes),
         out_shape=(
-            jax.ShapeDtypeStruct((1, pairs), f32),
-            jax.ShapeDtypeStruct((1, 1), f32),
-            jax.ShapeDtypeStruct((rows, model), bf16),
-            jax.ShapeDtypeStruct((share, width), f32),
-            jax.ShapeDtypeStruct((share, kv_width), f32),
-            jax.ShapeDtypeStruct((share, kv_width), f32),
-            jax.ShapeDtypeStruct((width, share), f32),
+            vmem((1, pairs), f32),
+            vmem((1, 1), f32),
+            vmem((rows, model), bf16),
+            vmem((share, width), f32),
+            vmem((share, kv_width), f32),
+            vmem((share, kv_width), f32),
+            vmem((share, width), f32),
         ),
-        in_specs=[VMEM_SPEC, smem_spec, smem_spec] + [VMEM_SPEC] * 9,
+        in_specs=[hbm_spec, smem_spec, smem_spec] + [hbm_spec] * 9,
         out_specs=(VMEM_SPEC,) * 7,
         scratch_shapes=[
-            vmem((share, width), bf16),
+            vmem((rows, model), bf16),
+        ]
+        + [vmem(a.shape, a.dtype) for a in operands[3:]]
+        + [
             vmem((model, width), bf16),
             vmem((model, kv_width), bf16),
             vmem((model, kv_width), bf16),
@@ -1009,8 +1072,8 @@
             vmem((count, 2 * slots, HEAD_WIDTH), bf16),
             vmem((count, slots, HEAD_WIDTH), bf16),
             vmem((count, slots, HEAD_WIDTH), bf16),
-            vmem((slots, HEAD_WIDTH), f32),
-            vmem((count, slots, HEAD_WIDTH), f32),
+            vmem((1, HEAD_WIDTH), f32),
+            vmem((count, 1, HEAD_WIDTH), f32),
             vmem((pb_count, line_count, 2, share, kv_width), bf16),
             vmem(block, bf16),
             vmem(block, bf16),
@@ -1022,15 +1085,16 @@
             dma((3,)),
             dma((pb_count,)),
             dma((pb_count,)),
-            dma((pb_count,)),
-            dma((pb_count,)),
+            dma((pb_count, line_count)),
+            dma((pb_count, line_count)),
             dma((line_count,)),
             dma((line_count,)),
             dma,
+            dma((pairs + 9,)),
         ]
         + gather_sems(pb_count, neg_count) * 6,
         compiler_params=pltpu.CompilerParams(
-            collective_id=0, has_side_effects=True, vmem_limit_bytes=60 * 2**20
+            collective_id=0, has_side_effects=True, vmem_limit_bytes=62 * 2**20
         ),
     )(*operands)
 
@@ -1067,7 +1131,7 @@
     )
     if own_kernels:
         cos_table, sin_table = signed_tables(seq_len, HEAD_WIDTH)
-        scores, loss, grad_rows, grad_query, grad_key, grad_value, grad_out = run_step(
+        results = run_step(
             (
                 hidden.reshape(pair_count * seq_len, model_width),
                 lengths,
@@ -1080,12 +1144,13 @@
                 query_weight,
                 key_matrix,
                 value_matrix,
-                out_weight,
+                out_weight.T,
             ),
             (pair_count, seq_len, group_count, share),
             pb_count,
             neg_count,
         )
+        scores, loss, grad_rows, grad_query, grad_key, grad_value, grad_out = write_outputs(results)
         return (
             scores,
             loss.reshape(()),
@@ -1093,7 +1158,7 @@
             grad_query,
             grad_key,
             grad_value,
-            grad_out,
+            grad_out.T,
         )
     packed = jnp.concatenate([query_weight, key_matrix, value_matrix, out_weight.T], axis=1)
     everything = lax.all_gather(packed, both, axis=0, tiled=True)

time: 88.6 us -> 78.4 us (0.88)
  local copies, waits for them, and re-layouts: 8.72 us -> 0 us
  between operations: 2.41 us -> 0.64 us
    unnamed x15 -> x0, local copies, waits for them, and re-layouts: 8.72 us -> none
    pallas_call x1 -> x2, Pallas kernels: 77.1 us -> 77.6 us  [the longest x1 75.3 us: run_step(): pl.pallas_call(functools.partial(step_kernel, sizes), out_shape=(vmem((1,...]
where the time goes in v2:
time: 78.4 us; the launch traced here: 78.2 us
  Pallas kernels  77.6 us (99%)
    pallas_call x1, Pallas kernels, run_step(): pl.pallas_call(functools.partial(step_kernel, sizes), out_shape=(vmem((1,...  75.3 us
    pallas_call x1, Pallas kernels, write_outputs(): pl.pallas_call(functools.partial(write_kernel, count), out_shape=tuple((j...  2.29 us

profile of v2, /device:TPU:0, one launch (start us, length us, event | category | flops | bytes accessed | tf_op | source)
XLA Modules:
  0.0 78.2 jit_solution(3829861091571907681)
XLA Ops:
  0.6 75.3 %shard_map.171 = (f32[1,4]{1,0:T(1,128)S(1)}, f32[1,1]{1,0:T(1,128)}, bf16[512,1024]{1,0:T(8,128)(2,1)S(1)}, f32[32,1024]{1,0:T(8,128)S(1)}, f32[32,512]{1,0:T(8...) custom-call(bf16[512,1024]{1,0:T(8,128)(2,1)} %bitcast.8, s32[1,4]{1,0:T(1,128)} %lengths.1, f32[1,4]{1,0:T(1,128)} %teacher.1, ...), custom_call_target="tpu_custom_call" | custom-call | tf_op jit(solution)/shard_map/pallas_call | solution.py:1031
  75.9 2.3 %shard_map.172 = (f32[1,4]{1,0:T(1,128)}, f32[1,1]{1,0:T(1,128)}, bf16[512,1024]{1,0:T(8,128)(2,1)}, f32[32,1024]{1,0:T(8,128)}, f32[32,512]{1,0:T(8,128)}, /*index=5*/f32[32,512]{1,0:T(8,128)}, f32[32,1024]{1,0:T(8,128)}) custom-call(f32[1,4]{1,0:T(1,128)S(1)} %get-tuple-element.21.refs_0_, f32[1,1]{1,0:T(1,128)} %get-tuple-element.22.refs_1_, ...), custom_call_target="tpu_custom_call" | custom-call | tf_op jit(solution)/shard_map/pallas_call | solution.py:1006

commit v3 on v2

--- a/solution.py
+++ b/solution.py
@@ -290,76 +290,76 @@
 
 def gather_sems(pb_count, neg_count):
     line_count = neg_count // 2
-    return [
-        pltpu.SemaphoreType.DMA((line_count,)),
-        pltpu.SemaphoreType.DMA((line_count,)),
-        pltpu.SemaphoreType.DMA((2, line_count)),
-        pltpu.SemaphoreType.DMA((2, line_count)),
-        pltpu.SemaphoreType.DMA((2, line_count)),
-        pltpu.SemaphoreType.DMA((2, line_count)),
-        pltpu.SemaphoreType.DMA((pb_count, line_count)),
-        pltpu.SemaphoreType.DMA((pb_count, line_count)),
-        pltpu.SemaphoreType.DMA,
-    ]
+    dma = pltpu.SemaphoreType.DMA
+    return [dma((line_count,)), dma((2, line_count)), dma((line_count,)), dma((2,))]
 
 
 class Gather:
-    def __init__(self, place, own, full, sems):
+    def __init__(self, place, own, full, sems, halve_corner):
         self.place, self.own, self.full = place, own, full
-        self.line_send, self.line_recv, self.pb_send, self.pb_recv = sems[:4]
-        self.half_send, self.half_recv = sems[4:6]
-        self.core_send, self.core_recv, self.local_sem = sems[6:]
-        self.sent = []
+        self.line_recv, self.pb_recv, self.corner_recv, ends = sems
+        self.send_sem, self.core_recv = ends.at[0], ends.at[1]
+        self.halve_corner = halve_corner
         across = place.pb + 1 - 2 * (place.pb % 2)
         along = place.pb + 2 - 4 * (place.pb // 2)
         self.near = (across, along)
         self.corner = 3 - place.pb
+        half = place.line // 2
+        self.is_inner = (place.line == 1) | (place.line == 2)
+        self.mate = place.line + 1 - 2 * (place.line % 2)
+        self.far_inner = 2 - half
+        self.far_outer = 3 - 3 * half
+        self.size = own.shape[0]
+        if halve_corner:
+            self.own_lines = (place.line, lax.rem(place.line + 2, 4))
+            self.mate_lines = (self.mate, lax.rem(self.mate + 2, 4))
+        else:
+            self.own_lines = (place.line, self.mate, self.far_inner, self.far_outer)
+            self.mate_lines = ()
 
     def rows(self, pb, line, core):
-        size = self.own.shape[0]
-        start = self.place.slot(pb, line, core) * size
-        return self.full.at[pl.ds(pl.multiple_of(start, size), size)]
-
-    def send(self, src, dst, send_sem, recv_sem, target):
-        copy = remote(src, dst, send_sem, recv_sem, target)
-        copy.start()
-        self.sent.append(copy)
+        start = self.place.slot(pb, line, core) * self.size
+        return self.full.at[pl.ds(pl.multiple_of(start, self.size), self.size)]
+
+    def blocks(self, count):
+        return self.full.at[pl.ds(0, count * self.size)]
+
+    def send(self, src, dst, recv_sem, target):
+        remote(src, dst, self.send_sem, recv_sem, target).start()
 
     def spread(self, src, line):
         at = self.place
         dst = self.rows(at.pb, line, at.core)
         for side in range(2):
-            self.send(
-                src, dst, self.pb_send.at[side, line], self.pb_recv.at[side, line], at.to_pb(self.near[side])
-            )
+            self.send(src, dst, self.pb_recv.at[side, line], at.to_pb(self.near[side]))
         self.pass_on(src, at.pb, line)
 
     def pass_on(self, src, pb, line):
         at = self.place
-        dst = self.rows(pb, line, at.core)
-        self.send(src, dst, self.core_send.at[pb, line], self.core_recv.at[pb, line], at.to_partner())
+        self.send(src, self.rows(pb, line, at.core), self.core_recv, at.to_partner())
 
     def arrive(self, block, recv_sem):
-        remote(block, block, self.local_sem, recv_sem, self.place.to_partner()).wait_recv()
+        remote(block, block, self.send_sem, recv_sem, self.place.to_partner()).wait_recv()
 
     def start(self):
         at = self.place
         mine = self.rows(at.pb, at.line, at.core)
-        self.local = pltpu.make_async_copy(self.own, mine, self.local_sem)
-        self.local.start()
-        for k in range(1, at.line_count):
-            line = at.line_peer(k)
-            self.send(
-                self.own, mine, self.line_send.at[k], self.line_recv.at[at.line], at.to_line(line)
-            )
+        for line in (self.mate, self.far_inner):
+            self.send(self.own, mine, self.line_recv.at[at.line], at.to_line(line))
         self.spread(self.own, at.line)
+        mine[...] = self.own[...]
 
     def middle(self):
         at = self.place
-        for k in range(1, at.line_count):
-            line = at.line_peer(k)
+        for line in (self.mate, self.far_inner, self.far_outer):
             block = self.rows(at.pb, line, at.core)
             self.arrive(block, self.line_recv.at[line])
+            if line is not self.mate:
+
+                @pl.when(self.is_inner)
+                def _():
+                    self.send(block, block, self.line_recv.at[line], at.to_line(self.mate))
+
             self.spread(block, line)
 
     def half(self, block, side):
@@ -368,37 +368,42 @@
 
     def relay(self):
         at = self.place
-        for step in range(at.line_count):
-            line = at.line_peer(step)
+        for line in self.own_lines + self.mate_lines:
             for side in range(2):
                 block = self.rows(self.near[side], line, at.core)
                 self.arrive(block, self.pb_recv.at[side, line])
-                part = self.half(block, side)
-                self.send(
-                    part,
-                    part,
-                    self.half_send.at[side, line],
-                    self.half_recv.at[side, line],
-                    at.to_pb(self.near[1 - side]),
-                )
+                if not any(line is other for other in self.mate_lines):
+                    part = self.half(block, side)
+                    self.send(part, part, self.corner_recv.at[line], at.to_pb(self.near[1 - side]))
                 self.pass_on(block, self.near[side], line)
+
+    def corner_in(self, lines, hand_over):
+        at = self.place
+        for line in lines:
+            block = self.rows(self.corner, line, at.core)
+            self.arrive(block, self.corner_recv.at[line])
+            if hand_over:
+                self.send(block, block, self.corner_recv.at[line], at.to_line(self.mate))
+            self.pass_on(block, self.corner, line)
+
+    def hand(self):
+        if self.halve_corner:
+            self.corner_in(self.own_lines, True)
 
     def finish(self):
         at = self.place
-        for step in range(at.line_count):
-            line = at.line_peer(step)
-            block = self.rows(self.corner, line, at.core)
-            for side in range(2):
-                self.arrive(self.half(block, side), self.half_recv.at[side, line])
-            self.pass_on(block, self.corner, line)
-        for pb in range(at.pb_count):
-            for line in range(at.line_count):
-                self.arrive(self.rows(pb, line, at.partner), self.core_recv.at[pb, line])
-        self.local.wait()
+        self.corner_in(self.mate_lines if self.halve_corner else self.own_lines, False)
+        self.arrive(self.blocks(at.count // 2), self.core_recv)
 
     def drain(self):
-        for copy in self.sent:
-            copy.wait_send()
+        at = self.place
+        block = self.blocks(at.count - 2)
+        remote(block, block, self.send_sem, self.core_recv, at.to_partner()).wait_send()
+
+        @pl.when(self.is_inner)
+        def _():
+            block = self.blocks(2)
+            remote(block, block, self.send_sem, self.core_recv, at.to_partner()).wait_send()
 
 
 VMEM_SPEC = pl.BlockSpec(memory_space=pltpu.VMEM)
@@ -568,21 +573,25 @@
         load.start()
         loads.append(load)
 
-    each = len(gather_sem_refs) // 6
-    gathers = []
-    for place_of, (own, full) in enumerate(
-        (
-            (own_k, full_k),
-            (own_v, full_v),
-            (own_q, full_q),
-            (own_o, full_o),
-            (context_own, context_full),
-            (late_own, late_full),
-        )
-    ):
-        sems = gather_sem_refs[place_of * each : (place_of + 1) * each]
-        gathers.append(Gather(at, own, full, sems))
-    gather_k, gather_v, gather_q, gather_o, gather_context, gather_late = gathers
+    half_width = own_q.shape[1] // 2
+    low, high = pl.ds(0, half_width), pl.ds(half_width, half_width)
+    parts = (
+        (own_k, full_k, True),
+        (own_v, full_v, True),
+        (own_q.at[:, low], full_q.at[:, low], True),
+        (own_q.at[:, high], full_q.at[:, high], True),
+        (own_o.at[:, low], full_o.at[:, low], True),
+        (own_o.at[:, high], full_o.at[:, high], False),
+        (context_own, context_full, False),
+        (late_own, late_full, False),
+    )
+    each = len(gather_sem_refs) // len(parts)
+    gathers = [
+        Gather(at, own, full, gather_sem_refs[i * each : (i + 1) * each], halve)
+        for i, (own, full, halve) in enumerate(parts)
+    ]
+    gather_k, gather_v, gather_q0, gather_q1, gather_o0, gather_o1 = gathers[:6]
+    gather_context, gather_late = gathers[6:]
 
     def norm_pair(pair, carry):
         rows = pl.ds(pl.multiple_of(pair * seq, seq), seq)
@@ -621,15 +630,17 @@
     sin_rows = jnp.concatenate([sin8] * groups, axis=0)
 
     pl.semaphore_wait(barrier, at.count - 1)
-    gather_k.start()
-    gather_v.start()
-    gather_q.start()
-    gather_o.start()
+    for gather in gathers[:6]:
+        gather.start()
     gather_k.middle()
     gather_v.middle()
     gather_k.relay()
-    gather_q.middle()
+    gather_q0.middle()
     gather_v.relay()
+    gather_k.hand()
+    gather_q1.middle()
+    gather_q0.relay()
+    gather_v.hand()
     gather_k.finish()
 
     def key_pair(pair, carry):
@@ -646,21 +657,30 @@
             key_rot[rows, lanes] = turned.astype(bf16)
         return carry
 
-    lax.fori_loop(0, pairs, key_pair, 0)
-
-    gather_o.middle()
-    gather_q.relay()
-    gather_v.finish()
-
     def value_pair(pair, carry):
         rows = pl.ds(pl.multiple_of(pair * seq, seq), seq)
         value_cast[rows, :] = mm(normed[rows, :], full_v[...]).astype(bf16)
         return carry
 
-    lax.fori_loop(0, pairs, value_pair, 0)
-
-    gather_o.relay()
-    gather_q.finish()
+    key_pair(0, 0)
+    gather_o0.middle()
+    key_pair(1, 0)
+    gather_q1.relay()
+    gather_q0.hand()
+    key_pair(2, 0)
+    gather_v.finish()
+    key_pair(3, 0)
+    gather_o1.middle()
+    gather_o0.relay()
+    gather_q1.hand()
+    value_pair(0, 0)
+    value_pair(1, 0)
+    gather_q0.finish()
+    gather_o1.relay()
+    gather_o0.hand()
+    value_pair(2, 0)
+    value_pair(3, 0)
+    gather_q1.finish()
 
     def stack_heads(wide):
         return jnp.concatenate(
@@ -743,7 +763,8 @@
     early = Exchange(at, early_src, early_dst, early_sems.at[0], early_sems.at[1])
     early.start()
 
-    gather_o.finish()
+    gather_o0.finish()
+    gather_o1.finish()
     attended = mm(context_wide, full_o[...], 1, 1)
     attended = attended + pltpu.roll(attended, pairs, 0)
     residual = x_last + attended
@@ -856,6 +877,7 @@
         arrive(from_core.at[pb], core_recv.at[pb])
         both = partial[pb, :, at.core].astype(f32) + from_core[pb].astype(f32)
         paired[pb] = both.astype(bf16)
+    gather_late.middle()
     for step in range(1, at.line_count + 1):
         line = at.line_peer(step % at.line_count)
         for k in range(1, at.pb_count):
@@ -875,10 +897,6 @@
             resid_src[index * turns + turn] = tile(packed, index)
     resid = Exchange(at, resid_src, resid_dst, resid_sems.at[0], resid_sems.at[1])
     resid.start()
-
-    gather_late.middle()
-    gather_late.relay()
-    gather_context.finish()
 
     back_last = mm(spread_heads(grad_q_cast.astype(f32)), full_q[...], 1, 1)
     last_grad[...] = back_last + pltpu.roll(back_last, pairs, 0)
@@ -932,6 +950,8 @@
     hidden_back(2, 0)
     for step in range(3, at.line_count + 1):
         own_sum = add_line(step)
+    gather_late.relay()
+    gather_context.finish()
     for pair in range(3, pairs):
         hidden_back(pair, 0)
 
@@ -1092,7 +1112,7 @@
             dma,
             dma((pairs + 9,)),
         ]
-        + gather_sems(pb_count, neg_count) * 6,
+        + gather_sems(pb_count, neg_count) * 8,
         compiler_params=pltpu.CompilerParams(
             collective_id=0, has_side_effects=True, vmem_limit_bytes=62 * 2**20
         ),
@@ -1120,7 +1140,7 @@
     group_count = kv_width // HEAD_WIDTH
     own_kernels = (
         pb_count == 4
-        and neg_count % 2 == 0
+        and neg_count == 8
         and share == out_share
         and share % 32 == 0
         and model_width == share * pb_count * neg_count

time: 78.4 us -> 72.4 us (0.923)
  Pallas kernels: 77.6 us -> 71.3 us
    pallas_call x1, Pallas kernels: 75.3 us -> 69 us  [run_step(): pl.pallas_call(functools.partial(step_kernel, sizes), out_shape=(vmem((1,...]
where the time goes in v3:
time: 72.4 us; the launch traced here: 72 us
  Pallas kernels  71.3 us (98%)
    pallas_call x1, Pallas kernels, run_step(): pl.pallas_call(functools.partial(step_kernel, sizes), out_shape=(vmem((1,...  69 us
    pallas_call x1, Pallas kernels, write_outputs(): pl.pallas_call(functools.partial(write_kernel, count), out_shape=tuple((j...  2.29 us

profile of v3, /device:TPU:0, one launch (start us, length us, event | category | flops | bytes accessed | tf_op | source)
XLA Modules:
  0.0 72.0 jit_solution(13847579058397986450)
XLA Ops:
  0.6 69.0 %shard_map.171 = (f32[1,4]{1,0:T(1,128)S(1)}, f32[1,1]{1,0:T(1,128)}, bf16[512,1024]{1,0:T(8,128)(2,1)S(1)}, f32[32,1024]{1,0:T(8,128)S(1)}, f32[32,512]{1,0:T(8...) custom-call(bf16[512,1024]{1,0:T(8,128)(2,1)} %bitcast.8, s32[1,4]{1,0:T(1,128)} %lengths.1, f32[1,4]{1,0:T(1,128)} %teacher.1, ...), custom_call_target="tpu_custom_call" | custom-call | tf_op jit(solution)/shard_map/pallas_call | solution.py:1051
  69.7 2.3 %shard_map.172 = (f32[1,4]{1,0:T(1,128)}, f32[1,1]{1,0:T(1,128)}, bf16[512,1024]{1,0:T(8,128)(2,1)}, f32[32,1024]{1,0:T(8,128)}, f32[32,512]{1,0:T(8,128)}, /*index=5*/f32[32,512]{1,0:T(8,128)}, f32[32,1024]{1,0:T(8,128)}) custom-call(f32[1,4]{1,0:T(1,128)S(1)} %get-tuple-element.21.refs_0_, f32[1,1]{1,0:T(1,128)} %get-tuple-element.22.refs_1_, ...), custom_call_target="tpu_custom_call" | custom-call | tf_op jit(solution)/shard_map/pallas_call | solution.py:1026

commit v4 on v3

--- a/solution.py
+++ b/solution.py
@@ -288,18 +288,20 @@
     )
 
 
-def gather_sems(pb_count, neg_count):
+def gather_sems(neg_count, large):
     line_count = neg_count // 2
     dma = pltpu.SemaphoreType.DMA
-    return [dma((line_count,)), dma((2, line_count)), dma((line_count,)), dma((2,))]
+    if large:
+        return [dma((line_count,)), dma((line_count,)), dma((line_count,)), dma((2,))]
+    return [dma((1,)), dma((1,)), dma((1,)), dma((2,))]
 
 
 class Gather:
-    def __init__(self, place, own, full, sems, halve_corner):
+    def __init__(self, place, own, full, sems, halve_corner, direct):
         self.place, self.own, self.full = place, own, full
         self.line_recv, self.pb_recv, self.corner_recv, ends = sems
         self.send_sem, self.core_recv = ends.at[0], ends.at[1]
-        self.halve_corner = halve_corner
+        self.halve_corner, self.direct = halve_corner, direct
         across = place.pb + 1 - 2 * (place.pb % 2)
         along = place.pb + 2 - 4 * (place.pb // 2)
         self.near = (across, along)
@@ -327,11 +329,14 @@
     def send(self, src, dst, recv_sem, target):
         remote(src, dst, self.send_sem, recv_sem, target).start()
 
+    def of(self, sems, line):
+        return sems.at[0] if self.direct else sems.at[line]
+
     def spread(self, src, line):
         at = self.place
         dst = self.rows(at.pb, line, at.core)
         for side in range(2):
-            self.send(src, dst, self.pb_recv.at[side, line], at.to_pb(self.near[side]))
+            self.send(src, dst, self.of(self.pb_recv, line), at.to_pb(self.near[side]))
         self.pass_on(src, at.pb, line)
 
     def pass_on(self, src, pb, line):
@@ -344,21 +349,25 @@
     def start(self):
         at = self.place
         mine = self.rows(at.pb, at.line, at.core)
-        for line in (self.mate, self.far_inner):
-            self.send(self.own, mine, self.line_recv.at[at.line], at.to_line(line))
+        peers = (self.mate, self.far_inner) + ((self.far_outer,) if self.direct else ())
+        for line in peers:
+            self.send(self.own, mine, self.of(self.line_recv, at.line), at.to_line(line))
         self.spread(self.own, at.line)
         mine[...] = self.own[...]
 
     def middle(self):
         at = self.place
+        if self.direct:
+            self.arrive(self.blocks(at.line_count - 1), self.line_recv.at[0])
         for line in (self.mate, self.far_inner, self.far_outer):
             block = self.rows(at.pb, line, at.core)
-            self.arrive(block, self.line_recv.at[line])
-            if line is not self.mate:
-
-                @pl.when(self.is_inner)
-                def _():
-                    self.send(block, block, self.line_recv.at[line], at.to_line(self.mate))
+            if not self.direct:
+                self.arrive(block, self.line_recv.at[line])
+                if line is not self.mate:
+
+                    @pl.when(self.is_inner)
+                    def _():
+                        self.send(block, block, self.line_recv.at[line], at.to_line(self.mate))
 
             self.spread(block, line)
 
@@ -368,20 +377,27 @@
 
     def relay(self):
         at = self.place
+        if self.direct:
+            self.arrive(self.blocks(2 * at.line_count), self.pb_recv.at[0])
         for line in self.own_lines + self.mate_lines:
+            if not self.direct:
+                self.arrive(self.blocks(2), self.pb_recv.at[line])
             for side in range(2):
                 block = self.rows(self.near[side], line, at.core)
-                self.arrive(block, self.pb_recv.at[side, line])
                 if not any(line is other for other in self.mate_lines):
                     part = self.half(block, side)
-                    self.send(part, part, self.corner_recv.at[line], at.to_pb(self.near[1 - side]))
+                    target = at.to_pb(self.near[1 - side])
+                    self.send(part, part, self.of(self.corner_recv, line), target)
                 self.pass_on(block, self.near[side], line)
 
     def corner_in(self, lines, hand_over):
         at = self.place
+        if self.direct:
+            self.arrive(self.blocks(at.line_count), self.corner_recv.at[0])
         for line in lines:
             block = self.rows(self.corner, line, at.core)
-            self.arrive(block, self.corner_recv.at[line])
+            if not self.direct:
+                self.arrive(block, self.corner_recv.at[line])
             if hand_over:
                 self.send(block, block, self.corner_recv.at[line], at.to_line(self.mate))
             self.pass_on(block, self.corner, line)
@@ -397,13 +413,14 @@
 
     def drain(self):
         at = self.place
-        block = self.blocks(at.count - 2)
+        block = self.blocks(at.count - (1 if self.direct else 2))
         remote(block, block, self.send_sem, self.core_recv, at.to_partner()).wait_send()
-
-        @pl.when(self.is_inner)
-        def _():
-            block = self.blocks(2)
-            remote(block, block, self.send_sem, self.core_recv, at.to_partner()).wait_send()
+        if not self.direct:
+
+            @pl.when(self.is_inner)
+            def _():
+                block = self.blocks(2)
+                remote(block, block, self.send_sem, self.core_recv, at.to_partner()).wait_send()
 
 
 VMEM_SPEC = pl.BlockSpec(memory_space=pltpu.VMEM)
@@ -483,6 +500,7 @@
     full_v,
     full_o,
     normed,
+    normed_t,
     inv_wide,
     key_unit,
     key_scale,
@@ -587,22 +605,28 @@
     )
     each = len(gather_sem_refs) // len(parts)
     gathers = [
-        Gather(at, own, full, gather_sem_refs[i * each : (i + 1) * each], halve)
+        Gather(at, own, full, gather_sem_refs[i * each : (i + 1) * each], halve, i >= 6)
         for i, (own, full, halve) in enumerate(parts)
     ]
     gather_k, gather_v, gather_q0, gather_q1, gather_o0, gather_o1 = gathers[:6]
     gather_context, gather_late = gathers[6:]
+
+    for load in small_loads:
+        load.wait()
+    pl.semaphore_wait(barrier, at.count - 1)
+    for gather in gathers[:4]:
+        gather.start()
 
     def norm_pair(pair, carry):
         rows = pl.ds(pl.multiple_of(pair * seq, seq), seq)
         wide = x[rows, :].astype(f32)
         inv = lax.rsqrt(lane_mean(wide * wide) + EPSILON)
         inv_wide[rows, :] = jnp.broadcast_to(inv, (seq, HEAD_WIDTH))
-        normed[rows, :] = (wide * inv * norm_gain[...]).astype(bf16)
+        scaled = wide * inv * norm_gain[...]
+        normed[rows, :] = scaled.astype(bf16)
+        normed_t[:, rows] = scaled.T.astype(bf16)
         return carry
 
-    for load in small_loads:
-        load.wait()
     for pair in range(pairs):
         loads[pair].wait()
         norm_pair(pair, 0)
@@ -629,20 +653,6 @@
     cos_rows = jnp.concatenate([cos8] * groups, axis=0)
     sin_rows = jnp.concatenate([sin8] * groups, axis=0)
 
-    pl.semaphore_wait(barrier, at.count - 1)
-    for gather in gathers[:6]:
-        gather.start()
-    gather_k.middle()
-    gather_v.middle()
-    gather_k.relay()
-    gather_q0.middle()
-    gather_v.relay()
-    gather_k.hand()
-    gather_q1.middle()
-    gather_q0.relay()
-    gather_v.hand()
-    gather_k.finish()
-
     def key_pair(pair, carry):
         rows = pl.ds(pl.multiple_of(pair * seq, seq), seq)
         proj = mm(normed[rows, :], full_k[...])
@@ -662,24 +672,34 @@
         value_cast[rows, :] = mm(normed[rows, :], full_v[...]).astype(bf16)
         return carry
 
-    key_pair(0, 0)
+    gather_k.middle()
+    gather_o0.start()
+    gather_o1.start()
+    gather_v.middle()
+    gather_q0.middle()
+    gather_k.relay()
+    gather_q1.middle()
+    gather_v.relay()
+    gather_k.hand()
     gather_o0.middle()
-    key_pair(1, 0)
+    gather_o1.middle()
+    gather_q0.relay()
+    gather_v.hand()
     gather_q1.relay()
     gather_q0.hand()
-    key_pair(2, 0)
-    gather_v.finish()
-    key_pair(3, 0)
-    gather_o1.middle()
+    gather_k.finish()
+    key_pair(0, 0)
+    key_pair(1, 0)
     gather_o0.relay()
     gather_q1.hand()
-    value_pair(0, 0)
-    value_pair(1, 0)
-    gather_q0.finish()
+    gather_v.finish()
+    key_pair(2, 0)
+    key_pair(3, 0)
     gather_o1.relay()
     gather_o0.hand()
-    value_pair(2, 0)
-    value_pair(3, 0)
+    for pair in range(pairs):
+        value_pair(pair, 0)
+    gather_q0.finish()
     gather_q1.finish()
 
     def stack_heads(wide):
@@ -791,7 +811,6 @@
     list_dst[at.me] = listing
     scores_out[...] = score_row[:, :pairs]
     gather_context.middle()
-    gather_context.relay()
 
     near_block = list_dst.at[pl.ds(0, at.neg_count - 1)]
     remote(near_block, near_block, list_sent, list_here, at.to_partner()).wait_recv()
@@ -832,6 +851,7 @@
     grad_q_cast = back_q.astype(bf16)
     late_own[stacked : 2 * stacked, :] = grad_q_cast
     gather_late.start()
+    gather_context.relay()
 
     def key_back(pair, carry):
         start = pl.multiple_of(pair * seq, seq)
@@ -846,28 +866,26 @@
             grad_k[rows, lanes] = back.astype(bf16)
         return carry
 
-    lax.fori_loop(0, pairs, key_back, 0)
+    for pair in range(pairs):
+        key_back(pair, 0)
 
     block_rows = model // at.pb_count
-    copies = []
 
     def send(src, dst, send_sem, recv_sem, target):
-        copy = remote(src, dst, send_sem, recv_sem, target)
-        copy.start()
-        copies.append(copy)
+        remote(src, dst, send_sem, recv_sem, target).start()
 
     def arrive(block, recv_sem):
         remote(block, block, any_sem, recv_sem, at.to_partner()).wait_recv()
 
     for k in range(1, at.pb_count + 1):
         pb = at.pb_peer(k % at.pb_count)
-        lanes = pl.ds(pl.multiple_of(pb * block_rows, block_rows), block_rows)
-        product = mm(normed[:, lanes], grad_k[...], 0, 0)
+        chosen = pl.ds(pl.multiple_of(pb * block_rows, block_rows), block_rows)
+        product = mm(normed_t[chosen, :], grad_k[...])
         partial[pb] = product.astype(bf16).reshape(at.line_count, 2, share, kv_width)
         send(
             partial.at[pb, :, at.partner],
             from_core.at[pb],
-            core_send.at[pb],
+            core_send,
             core_recv.at[pb],
             at.to_partner(),
         )
@@ -885,8 +903,8 @@
             send(
                 paired.at[pb, line],
                 from_pb.at[at.pb, line],
-                pb_send.at[k, line],
-                pb_recv.at[at.pb, line],
+                pb_send,
+                pb_recv.at[line],
                 at.to_pb(pb),
             )
 
@@ -928,30 +946,30 @@
     def add_line(step):
         line = at.line_peer(step % at.line_count)
         total = paired[at.pb, line].astype(f32)
+        arrive(from_pb.at[pl.ds(0, at.pb_count - 1), line], pb_recv.at[line])
         for k in range(1, at.pb_count):
             pb = at.pb_peer(k)
-            arrive(from_pb.at[pb, line], pb_recv.at[pb, line])
             total = total + from_pb[pb, line].astype(f32)
         if step < at.line_count:
             summed[line] = total.astype(bf16)
             send(
                 summed.at[line],
                 from_line.at[at.line],
-                line_send.at[line],
-                line_recv.at[at.line],
+                line_send,
+                line_recv,
                 at.to_line(line),
             )
         return total
 
     hidden_back(0, 0)
     add_line(1)
+    gather_late.relay()
     hidden_back(1, 0)
     add_line(2)
+    gather_context.finish()
     hidden_back(2, 0)
     for step in range(3, at.line_count + 1):
         own_sum = add_line(step)
-    gather_late.relay()
-    gather_context.finish()
     for pair in range(3, pairs):
         hidden_back(pair, 0)
 
@@ -992,16 +1010,21 @@
             ]
 
     final = own_sum
+    arrive(from_line.at[pl.ds(0, at.line_count - 1)], line_recv)
     for step in range(1, at.line_count):
         line = at.line_peer(step)
-        arrive(from_line.at[line], line_recv.at[line])
         final = final + from_line[line].astype(f32)
     grad_key[...] = final
 
     for gather in gathers:
         gather.drain()
-    for copy in copies:
-        copy.wait_send()
+    pieces = from_line.at[pl.ds(0, at.line_count - 1)]
+    for block, sem in (
+        (from_core, core_send),
+        (from_pb.at[pl.ds(0, at.pb_count - 1)], pb_send),
+        (pieces, line_send),
+    ):
+        remote(block, block, sem, any_sem, at.to_partner()).wait_send()
     early.wait("wait_send")
     resid.wait("wait_send")
     sent_block = list_dst.at[pl.ds(0, at.count - 1)]
@@ -1071,6 +1094,7 @@
             vmem((model, kv_width), bf16),
             vmem((model, width), bf16),
             vmem((rows, model), bf16),
+            vmem((model, rows), bf16),
             vmem((rows, HEAD_WIDTH), f32),
             vmem((rows, kv_width), f32),
             vmem((rows, kv_width), f32),
@@ -1103,16 +1127,17 @@
             dma((2,)),
             dma((2,)),
             dma((3,)),
+            dma,
             dma((pb_count,)),
-            dma((pb_count,)),
-            dma((pb_count, line_count)),
-            dma((pb_count, line_count)),
+            dma,
             dma((line_count,)),
-            dma((line_count,)),
+            dma,
+            dma,
             dma,
             dma((pairs + 9,)),
         ]
-        + gather_sems(pb_count, neg_count) * 8,
+        + gather_sems(neg_count, True) * 6
+        + gather_sems(neg_count, False) * 2,
         compiler_params=pltpu.CompilerParams(
             collective_id=0, has_side_effects=True, vmem_limit_bytes=62 * 2**20
         ),

time: 72.4 us -> 67.8 us (0.936)
  Pallas kernels: 71.3 us -> 66.9 us
    pallas_call x1, Pallas kernels: 69 us -> 64.6 us  [run_step(): pl.pallas_call(functools.partial(step_kernel, sizes), out_shape=(vmem((1,...]
where the time goes in v4:
time: 67.8 us; the launch traced here: 67.7 us
  Pallas kernels  66.9 us (99%)
  between operations  0.8 us (1%)
    pallas_call x1, Pallas kernels, run_step(): pl.pallas_call(functools.partial(step_kernel, sizes), out_shape=(vmem((1,...  64.6 us
    pallas_call x1, Pallas kernels, write_outputs(): pl.pallas_call(functools.partial(write_kernel, count), out_shape=tuple((j...  2.29 us

profile of v4, /device:TPU:0, one launch (start us, length us, event | category | flops | bytes accessed | tf_op | source)
XLA Modules:
  0.0 67.7 jit_solution(16838427350122365946)
XLA Ops:
  0.6 64.6 %shard_map.171 = (f32[1,4]{1,0:T(1,128)S(1)}, f32[1,1]{1,0:T(1,128)}, bf16[512,1024]{1,0:T(8,128)(2,1)S(1)}, f32[32,1024]{1,0:T(8,128)S(1)}, f32[32,512]{1,0:T(8...) custom-call(bf16[512,1024]{1,0:T(8,128)(2,1)} %bitcast.8, s32[1,4]{1,0:T(1,128)} %lengths.1, f32[1,4]{1,0:T(1,128)} %teacher.1, ...), custom_call_target="tpu_custom_call" | custom-call | tf_op jit(solution)/shard_map/pallas_call | solution.py:1074
  65.2 2.3 %shard_map.172 = (f32[1,4]{1,0:T(1,128)}, f32[1,1]{1,0:T(1,128)}, bf16[512,1024]{1,0:T(8,128)(2,1)}, f32[32,1024]{1,0:T(8,128)}, f32[32,512]{1,0:T(8,128)}, /*index=5*/f32[32,512]{1,0:T(8,128)}, f32[32,1024]{1,0:T(8,128)}) custom-call(f32[1,4]{1,0:T(1,128)S(1)} %get-tuple-element.21.refs_0_, f32[1,1]{1,0:T(1,128)} %get-tuple-element.22.refs_1_, ...), custom_call_target="tpu_custom_call" | custom-call | tf_op jit(solution)/shard_map/pallas_call | solution.py:1049

commit v5 on v4

--- a/solution.py
+++ b/solution.py
@@ -406,10 +406,11 @@
         if self.halve_corner:
             self.corner_in(self.own_lines, True)
 
+    def tail(self):
+        self.corner_in(self.mate_lines if self.halve_corner else self.own_lines, False)
+
     def finish(self):
-        at = self.place
-        self.corner_in(self.mate_lines if self.halve_corner else self.own_lines, False)
-        self.arrive(self.blocks(at.count // 2), self.core_recv)
+        self.arrive(self.blocks(self.place.count // 2), self.core_recv)
 
     def drain(self):
         at = self.place
@@ -687,18 +688,23 @@
     gather_v.hand()
     gather_q1.relay()
     gather_q0.hand()
+    gather_k.tail()
+    gather_o0.relay()
+    gather_q1.hand()
+    gather_v.tail()
     gather_k.finish()
     key_pair(0, 0)
     key_pair(1, 0)
-    gather_o0.relay()
-    gather_q1.hand()
-    gather_v.finish()
+    gather_o1.relay()
+    gather_o0.hand()
+    gather_q0.tail()
     key_pair(2, 0)
     key_pair(3, 0)
-    gather_o1.relay()
-    gather_o0.hand()
+    gather_q1.tail()
+    gather_v.finish()
     for pair in range(pairs):
         value_pair(pair, 0)
+    gather_o0.tail()
     gather_q0.finish()
     gather_q1.finish()
 
@@ -754,6 +760,7 @@
     context_own[...] = context.astype(bf16)
     context_wide = spread_heads(context)
     gather_context.start()
+    gather_o1.tail()
 
     lane_block = lax.rem(
         lax.broadcasted_iota(jnp.int32, (slots, model), 1) // share, HEAD_WIDTH // share
@@ -853,23 +860,27 @@
     gather_late.start()
     gather_context.relay()
 
-    def key_back(pair, carry):
-        start = pl.multiple_of(pair * seq, seq)
-        rows = pl.ds(start, seq)
-        turned = mm(logit_grad[:, rows], query_blocks[...], 0, 0) * HEAD_WIDTH ** (-0.5)
-        for group in range(groups):
-            lanes = slice(group * HEAD_WIDTH, (group + 1) * HEAD_WIDTH)
-            part = turned[:, lanes]
-            unit = key_unit[rows, lanes]
-            back = part * cos_table[...] - pltpu.roll(part, HEAD_WIDTH // 2, 1) * sin_table[...]
-            back = key_scale[rows, lanes] * (back - unit * lane_mean(back * unit))
-            grad_k[rows, lanes] = back.astype(bf16)
-        return carry
-
-    for pair in range(pairs):
-        key_back(pair, 0)
-
+    cuts = 2
+    cut_width = kv_width // cuts
     block_rows = model // at.pb_count
+
+    def key_back(cut):
+        columns = slice(cut * cut_width, (cut + 1) * cut_width)
+
+        def one(pair, carry):
+            rows = pl.ds(pl.multiple_of(pair * seq, seq), seq)
+            turned = mm(logit_grad[:, rows], query_blocks[:, columns], 0, 0) * HEAD_WIDTH ** (-0.5)
+            for group in range(groups // cuts):
+                start = cut * cut_width + group * HEAD_WIDTH
+                lanes = slice(start, start + HEAD_WIDTH)
+                part = tile(turned, group)
+                unit = key_unit[rows, lanes]
+                back = part * cos_table[...] - pltpu.roll(part, HEAD_WIDTH // 2, 1) * sin_table[...]
+                back = key_scale[rows, lanes] * (back - unit * lane_mean(back * unit))
+                grad_k[rows, lanes] = back.astype(bf16)
+            return carry
+
+        lax.fori_loop(0, pairs, one, 0)
 
     def send(src, dst, send_sem, recv_sem, target):
         remote(src, dst, send_sem, recv_sem, target).start()
@@ -877,36 +888,46 @@
     def arrive(block, recv_sem):
         remote(block, block, any_sem, recv_sem, at.to_partner()).wait_recv()
 
-    for k in range(1, at.pb_count + 1):
-        pb = at.pb_peer(k % at.pb_count)
-        chosen = pl.ds(pl.multiple_of(pb * block_rows, block_rows), block_rows)
-        product = mm(normed_t[chosen, :], grad_k[...])
-        partial[pb] = product.astype(bf16).reshape(at.line_count, 2, share, kv_width)
-        send(
-            partial.at[pb, :, at.partner],
-            from_core.at[pb],
-            core_send,
-            core_recv.at[pb],
-            at.to_partner(),
-        )
-
-    for k in range(1, at.pb_count + 1):
-        pb = at.pb_peer(k % at.pb_count)
-        arrive(from_core.at[pb], core_recv.at[pb])
-        both = partial[pb, :, at.core].astype(f32) + from_core[pb].astype(f32)
-        paired[pb] = both.astype(bf16)
+    def key_products(cut):
+        columns = slice(cut * cut_width, (cut + 1) * cut_width)
+        for k in range(1, at.pb_count + 1):
+            pb = at.pb_peer(k % at.pb_count)
+            chosen = pl.ds(pl.multiple_of(pb * block_rows, block_rows), block_rows)
+            product = mm(normed_t[chosen, :], grad_k[:, columns])
+            partial[cut, pb] = product.astype(bf16).reshape(at.line_count, 2, share, cut_width)
+            send(
+                partial.at[cut, pb, :, at.partner],
+                from_core.at[cut, pb],
+                core_send,
+                core_recv.at[cut, pb],
+                at.to_partner(),
+            )
+
+    def key_pairs(cut):
+        for k in range(1, at.pb_count + 1):
+            pb = at.pb_peer(k % at.pb_count)
+            arrive(from_core.at[cut, pb], core_recv.at[cut, pb])
+            both = partial[cut, pb, :, at.core].astype(f32) + from_core[cut, pb].astype(f32)
+            paired[pb, :, cut] = both.astype(bf16)
+        for step in range(1, at.line_count + 1):
+            line = at.line_peer(step % at.line_count)
+            for k in range(1, at.pb_count):
+                pb = at.pb_peer(k)
+                send(
+                    paired.at[pb, line, cut],
+                    from_pb.at[at.pb, line, cut],
+                    pb_send,
+                    pb_recv.at[line],
+                    at.to_pb(pb),
+                )
+
+    key_back(0)
+    key_products(0)
+    key_back(1)
+    key_pairs(0)
+    key_products(1)
     gather_late.middle()
-    for step in range(1, at.line_count + 1):
-        line = at.line_peer(step % at.line_count)
-        for k in range(1, at.pb_count):
-            pb = at.pb_peer(k)
-            send(
-                paired.at[pb, line],
-                from_pb.at[at.pb, line],
-                pb_send,
-                pb_recv.at[line],
-                at.to_pb(pb),
-            )
+    key_pairs(1)
 
     resid_parts = by_head(resid_cast.astype(f32))
     for turn in range(turns):
@@ -966,10 +987,11 @@
     gather_late.relay()
     hidden_back(1, 0)
     add_line(2)
-    gather_context.finish()
+    gather_context.tail()
     hidden_back(2, 0)
     for step in range(3, at.line_count + 1):
         own_sum = add_line(step)
+    gather_late.tail()
     for pair in range(3, pairs):
         hidden_back(pair, 0)
 
@@ -981,6 +1003,7 @@
         loss = loss + total(expo_t / sum_t * (scaled - jnp.log(sum_t) - (score - jnp.log(sum_s))))
     loss_out[...] = loss
 
+    gather_context.finish()
     gather_late.finish()
     early.wait("wait_recv")
     resid.wait("wait_recv")
@@ -1014,7 +1037,8 @@
     for step in range(1, at.line_count):
         line = at.line_peer(step)
         final = final + from_line[line].astype(f32)
-    grad_key[...] = final
+    for cut in range(cuts):
+        grad_key[:, cut * cut_width : (cut + 1) * cut_width] = final[cut]
 
     for gather in gathers:
         gather.drain()
@@ -1066,7 +1090,7 @@
     slots = width // kv_width * pairs
     stacked = groups * slots
     bf16, f32 = jnp.bfloat16, jnp.float32
-    block = (pb_count, line_count, share, kv_width)
+    block = (pb_count, line_count, 2, share, kv_width // 2)
     dma = pltpu.SemaphoreType.DMA
     vmem = pltpu.VMEM
     smem_spec = pl.BlockSpec(memory_space=pltpu.SMEM)
@@ -1118,8 +1142,8 @@
             vmem((count, slots, HEAD_WIDTH), bf16),
             vmem((1, HEAD_WIDTH), f32),
             vmem((count, 1, HEAD_WIDTH), f32),
-            vmem((pb_count, line_count, 2, share, kv_width), bf16),
-            vmem(block, bf16),
+            vmem((2, pb_count, line_count, 2, share, kv_width // 2), bf16),
+            vmem((2, pb_count, line_count, share, kv_width // 2), bf16),
             vmem(block, bf16),
             vmem(block, bf16),
             vmem(block[1:], bf16),
@@ -1128,7 +1152,7 @@
             dma((2,)),
             dma((3,)),
             dma,
-            dma((pb_count,)),
+            dma((2, pb_count)),
             dma,
             dma((line_count,)),
             dma,

time: 67.8 us -> 66.3 us (0.978)
  Pallas kernels: 66.9 us -> 65.3 us
    pallas_call x1, Pallas kernels: 64.6 us -> 63 us  [run_step(): pl.pallas_call(functools.partial(step_kernel, sizes), out_shape=(vmem((1,...]
where the time goes in v5:
time: 66.3 us; the launch traced here: 66.1 us
  Pallas kernels  65.3 us (98%)
  between operations  0.8 us (1%)
    pallas_call x1, Pallas kernels, run_step(): pl.pallas_call(functools.partial(step_kernel, sizes), out_shape=(vmem((1,...  63 us
    pallas_call x1, Pallas kernels, write_outputs(): pl.pallas_call(functools.partial(write_kernel, count), out_shape=tuple((j...  2.29 us

profile of v5, /device:TPU:0, one launch (start us, length us, event | category | flops | bytes accessed | tf_op | source)
XLA Modules:
  0.0 66.1 jit_solution(7345101158358170493)
XLA Ops:
  0.6 63.0 %shard_map.171 = (f32[1,4]{1,0:T(1,128)S(1)}, f32[1,1]{1,0:T(1,128)}, bf16[512,1024]{1,0:T(8,128)(2,1)S(1)}, f32[32,1024]{1,0:T(8,128)S(1)}, f32[32,512]{1,0:T(8...) custom-call(bf16[512,1024]{1,0:T(8,128)(2,1)} %bitcast.8, s32[1,4]{1,0:T(1,128)} %lengths.1, f32[1,4]{1,0:T(1,128)} %teacher.1, ...), custom_call_target="tpu_custom_call" | custom-call | tf_op jit(solution)/shard_map/pallas_call | solution.py:1098
  63.7 2.3 %shard_map.172 = (f32[1,4]{1,0:T(1,128)}, f32[1,1]{1,0:T(1,128)}, bf16[512,1024]{1,0:T(8,128)(2,1)}, f32[32,1024]{1,0:T(8,128)}, f32[32,512]{1,0:T(8,128)}, /*index=5*/f32[32,512]{1,0:T(8,128)}, f32[32,1024]{1,0:T(8,128)}) custom-call(f32[1,4]{1,0:T(1,128)S(1)} %get-tuple-element.21.refs_0_, f32[1,1]{1,0:T(1,128)} %get-tuple-element.22.refs_1_, ...), custom_call_target="tpu_custom_call" | custom-call | tf_op jit(solution)/shard_map/pallas_call | solution.py:1073

commit v6 on v5

--- a/solution.py
+++ b/solution.py
@@ -692,14 +692,12 @@
     gather_o0.relay()
     gather_q1.hand()
     gather_v.tail()
-    gather_k.finish()
-    key_pair(0, 0)
-    key_pair(1, 0)
     gather_o1.relay()
     gather_o0.hand()
     gather_q0.tail()
-    key_pair(2, 0)
-    key_pair(3, 0)
+    gather_k.finish()
+    for pair in range(pairs):
+        key_pair(pair, 0)
     gather_q1.tail()
     gather_v.finish()
     for pair in range(pairs):
@@ -755,7 +753,7 @@
     expos = jnp.where(visible, jnp.exp(logits), 0.0)
     attention_weights = expos / jnp.sum(expos, axis=-1, keepdims=True)
     probs = attention_weights.astype(bf16)
-    probs_ref[...] = probs
+    probs_ref[...] = attention_weights.T.astype(bf16)
     context = diagonal_of(mm(probs, value_cast[...]))
     context_own[...] = context.astype(bf16)
     context_wide = spread_heads(context)
@@ -850,7 +848,7 @@
     grad_probs = mm(context_blocks[...], value_cast[...], 1, 1)
     spread = jnp.sum(attention_weights * grad_probs, axis=-1, keepdims=True)
     logit_gradient = (attention_weights * (grad_probs - spread)).astype(bf16)
-    logit_grad[...] = logit_gradient
+    logit_grad[...] = (attention_weights * (grad_probs - spread)).T.astype(bf16)
 
     turned_q = diagonal_of(mm(logit_gradient, key_rot[...])) * HEAD_WIDTH ** (-0.5)
     back_q = turned_q * cos_rows - pltpu.roll(turned_q, HEAD_WIDTH // 2, 1) * sin_rows
@@ -860,7 +858,7 @@
     gather_late.start()
     gather_context.relay()
 
-    cuts = 2
+    cuts = 1
     cut_width = kv_width // cuts
     block_rows = model // at.pb_count
 
@@ -869,7 +867,7 @@
 
         def one(pair, carry):
             rows = pl.ds(pl.multiple_of(pair * seq, seq), seq)
-            turned = mm(logit_grad[:, rows], query_blocks[:, columns], 0, 0) * HEAD_WIDTH ** (-0.5)
+            turned = mm(logit_grad[rows, :], query_blocks[:, columns]) * HEAD_WIDTH ** (-0.5)
             for group in range(groups // cuts):
                 start = cut * cut_width + group * HEAD_WIDTH
                 lanes = slice(start, start + HEAD_WIDTH)
@@ -904,11 +902,13 @@
             )
 
     def key_pairs(cut):
-        for k in range(1, at.pb_count + 1):
-            pb = at.pb_peer(k % at.pb_count)
+        def add_pair(pb):
             arrive(from_core.at[cut, pb], core_recv.at[cut, pb])
             both = partial[cut, pb, :, at.core].astype(f32) + from_core[cut, pb].astype(f32)
             paired[pb, :, cut] = both.astype(bf16)
+
+        for k in range(1, at.pb_count):
+            add_pair(at.pb_peer(k))
         for step in range(1, at.line_count + 1):
             line = at.line_peer(step % at.line_count)
             for k in range(1, at.pb_count):
@@ -920,14 +920,12 @@
                     pb_recv.at[line],
                     at.to_pb(pb),
                 )
+        add_pair(at.pb)
 
     key_back(0)
     key_products(0)
-    key_back(1)
+    gather_late.middle()
     key_pairs(0)
-    key_products(1)
-    gather_late.middle()
-    key_pairs(1)
 
     resid_parts = by_head(resid_cast.astype(f32))
     for turn in range(turns):
@@ -943,7 +941,7 @@
     def value_back(pair, carry):
         start = pl.multiple_of(pair * seq, seq)
         rows = pl.ds(start, seq)
-        grad_v[rows, :] = mm(probs_ref[:, rows], context_blocks[...], 0, 0).astype(bf16)
+        grad_v[rows, :] = mm(probs_ref[rows, :], context_blocks[...]).astype(bf16)
         return carry
 
     lax.fori_loop(0, pairs, value_back, 0)
@@ -983,9 +981,18 @@
         return total
 
     hidden_back(0, 0)
+    hidden_back(1, 0)
     add_line(1)
     gather_late.relay()
-    hidden_back(1, 0)
+
+    far_block = list_dst.at[pl.ds(0, at.count - at.neg_count)]
+    remote(far_block, far_block, list_sent, list_there, at.to_partner()).wait_recv()
+    loss = jnp.zeros((1, 1), f32)
+    for pb in range(at.pb_count):
+        score, scaled, expo_t, sum_s, sum_t = query_terms(pb * at.neg_count)
+        loss = loss + total(expo_t / sum_t * (scaled - jnp.log(sum_t) - (score - jnp.log(sum_s))))
+    loss_out[...] = loss
+
     add_line(2)
     gather_context.tail()
     hidden_back(2, 0)
@@ -994,14 +1001,6 @@
     gather_late.tail()
     for pair in range(3, pairs):
         hidden_back(pair, 0)
-
-    far_block = list_dst.at[pl.ds(0, at.count - at.neg_count)]
-    remote(far_block, far_block, list_sent, list_there, at.to_partner()).wait_recv()
-    loss = jnp.zeros((1, 1), f32)
-    for pb in range(at.pb_count):
-        score, scaled, expo_t, sum_s, sum_t = query_terms(pb * at.neg_count)
-        loss = loss + total(expo_t / sum_t * (scaled - jnp.log(sum_t) - (score - jnp.log(sum_s))))
-    loss_out[...] = loss
 
     gather_context.finish()
     gather_late.finish()
@@ -1090,7 +1089,7 @@
     slots = width // kv_width * pairs
     stacked = groups * slots
     bf16, f32 = jnp.bfloat16, jnp.float32
-    block = (pb_count, line_count, 2, share, kv_width // 2)
+    block = (pb_count, line_count, 1, share, kv_width)
     dma = pltpu.SemaphoreType.DMA
     vmem = pltpu.VMEM
     smem_spec = pl.BlockSpec(memory_space=pltpu.SMEM)
@@ -1126,8 +1125,8 @@
             vmem((rows, kv_width), bf16),
             vmem((rows, kv_width), bf16),
             vmem((rows, kv_width), bf16),
-            vmem((stacked, rows), bf16),
-            vmem((stacked, rows), bf16),
+            vmem((rows, stacked), bf16),
+            vmem((rows, stacked), bf16),
             vmem((stacked, kv_width), bf16),
             vmem((stacked, kv_width), bf16),
             vmem((slots, model), f32),
@@ -1142,8 +1141,8 @@
             vmem((count, slots, HEAD_WIDTH), bf16),
             vmem((1, HEAD_WIDTH), f32),
             vmem((count, 1, HEAD_WIDTH), f32),
-            vmem((2, pb_count, line_count, 2, share, kv_width // 2), bf16),
-            vmem((2, pb_count, line_count, share, kv_width // 2), bf16),
+            vmem((1, pb_count, line_count, 2, share, kv_width), bf16),
+            vmem((1, pb_count, line_count, share, kv_width), bf16),
             vmem(block, bf16),
             vmem(block, bf16),
             vmem(block[1:], bf16),
@@ -1152,7 +1151,7 @@
             dma((2,)),
             dma((3,)),
             dma,
-            dma((2, pb_count)),
+            dma((1, pb_count)),
             dma,
             dma((line_count,)),
             dma,

time: 66.3 us -> 64.5 us (0.973)
  Pallas kernels: 65.3 us -> 63.7 us
    pallas_call x1, Pallas kernels: 63 us -> 61.4 us  [run_step(): pl.pallas_call(functools.partial(step_kernel, sizes), out_shape=(vmem((1,...]
where the time goes in v6:
time: 64.5 us; the launch traced here: 64.4 us
  Pallas kernels  63.7 us (99%)
    pallas_call x1, Pallas kernels, run_step(): pl.pallas_call(functools.partial(step_kernel, sizes), out_shape=(vmem((1,...  61.4 us
    pallas_call x1, Pallas kernels, write_outputs(): pl.pallas_call(functools.partial(write_kernel, count), out_shape=tuple((j...  2.29 us

profile of v6, /device:TPU:0, one launch (start us, length us, event | category | flops | bytes accessed | tf_op | source)
XLA Modules:
  0.0 64.4 jit_solution(15204178038187158745)
XLA Ops:
  0.6 61.4 %shard_map.171 = (f32[1,4]{1,0:T(1,128)S(1)}, f32[1,1]{1,0:T(1,128)}, bf16[512,1024]{1,0:T(8,128)(2,1)S(1)}, f32[32,1024]{1,0:T(8,128)S(1)}, f32[32,512]{1,0:T(8...) custom-call(bf16[512,1024]{1,0:T(8,128)(2,1)} %bitcast.8, s32[1,4]{1,0:T(1,128)} %lengths.1, f32[1,4]{1,0:T(1,128)} %teacher.1, ...), custom_call_target="tpu_custom_call" | custom-call | tf_op jit(solution)/shard_map/pallas_call | solution.py:1097
  62.1 2.3 %shard_map.172 = (f32[1,4]{1,0:T(1,128)}, f32[1,1]{1,0:T(1,128)}, bf16[512,1024]{1,0:T(8,128)(2,1)}, f32[32,1024]{1,0:T(8,128)}, f32[32,512]{1,0:T(8,128)}, /*index=5*/f32[32,512]{1,0:T(8,128)}, f32[32,1024]{1,0:T(8,128)}) custom-call(f32[1,4]{1,0:T(1,128)S(1)} %get-tuple-element.21.refs_0_, f32[1,1]{1,0:T(1,128)} %get-tuple-element.22.refs_1_, ...), custom_call_target="tpu_custom_call" | custom-call | tf_op jit(solution)/shard_map/pallas_call | solution.py:1072

commit v7 on v6

--- a/solution.py
+++ b/solution.py
@@ -695,16 +695,17 @@
     gather_o1.relay()
     gather_o0.hand()
     gather_q0.tail()
+    gather_q1.tail()
     gather_k.finish()
     for pair in range(pairs):
         key_pair(pair, 0)
-    gather_q1.tail()
     gather_v.finish()
     for pair in range(pairs):
         value_pair(pair, 0)
     gather_o0.tail()
     gather_q0.finish()
     gather_q1.finish()
+    gather_o1.tail()
 
     def stack_heads(wide):
         return jnp.concatenate(
@@ -758,7 +759,6 @@
     context_own[...] = context.astype(bf16)
     context_wide = spread_heads(context)
     gather_context.start()
-    gather_o1.tail()
 
     lane_block = lax.rem(
         lax.broadcasted_iota(jnp.int32, (slots, model), 1) // share, HEAD_WIDTH // share
@@ -776,21 +776,10 @@
         return [jnp.where(upper8, wide, 0.0), jnp.where(upper8, 0.0, wide)]
 
     turns = HEAD_WIDTH // share
-    pulled = mm(probs, normed[...])
-    pulled_parts = [pulled[group * slots : (group + 1) * slots] for group in range(groups)]
-    last_parts = by_head(normed_last.astype(f32))
-    for turn in range(turns):
-        both = jnp.concatenate([pack(pulled_parts, turn), pack(last_parts, turn)], axis=0)
-        both = both.astype(bf16)
-        for index in range(model // HEAD_WIDTH):
-            early_src[index * turns + turn] = tile(both, index)
-
-    early = Exchange(at, early_src, early_dst, early_sems.at[0], early_sems.at[1])
-    early.start()
-
     gather_o0.finish()
+    attended = mm(context_wide[:, :half_width], full_o[:, :half_width], 1, 1)
     gather_o1.finish()
-    attended = mm(context_wide, full_o[...], 1, 1)
+    attended = attended + mm(context_wide[:, half_width:], full_o[:, half_width:], 1, 1)
     attended = attended + pltpu.roll(attended, pairs, 0)
     residual = x_last + attended
     out_scale = lax.rsqrt(lane_mean(residual * residual) + EPSILON)
@@ -815,6 +804,18 @@
         remote(list_src, me_row, list_sent, arrived, target).start()
     list_dst[at.me] = listing
     scores_out[...] = score_row[:, :pairs]
+
+    pulled = mm(probs, normed[...])
+    pulled_parts = [pulled[group * slots : (group + 1) * slots] for group in range(groups)]
+    last_parts = by_head(normed_last.astype(f32))
+    for turn in range(turns):
+        both = jnp.concatenate([pack(pulled_parts, turn), pack(last_parts, turn)], axis=0)
+        both = both.astype(bf16)
+        for index in range(model // HEAD_WIDTH):
+            early_src[index * turns + turn] = tile(both, index)
+
+    early = Exchange(at, early_src, early_dst, early_sems.at[0], early_sems.at[1])
+    early.start()
     gather_context.middle()
 
     near_block = list_dst.at[pl.ds(0, at.neg_count - 1)]
@@ -982,6 +983,7 @@
 
     hidden_back(0, 0)
     hidden_back(1, 0)
+    hidden_back(2, 0)
     add_line(1)
     gather_late.relay()
 
@@ -995,7 +997,6 @@
 
     add_line(2)
     gather_context.tail()
-    hidden_back(2, 0)
     for step in range(3, at.line_count + 1):
         own_sum = add_line(step)
     gather_late.tail()

time: 64.5 us -> 63.8 us (0.989)
  Pallas kernels: 63.7 us -> 63 us
    pallas_call x1, Pallas kernels: 61.4 us -> 60.7 us  [run_step(): pl.pallas_call(functools.partial(step_kernel, sizes), out_shape=(vmem((1,...]
where the time goes in v7:
time: 63.8 us; the launch traced here: 63.7 us
  Pallas kernels  63 us (99%)
  between operations  0.64 us (1%)
    pallas_call x1, Pallas kernels, run_step(): pl.pallas_call(functools.partial(step_kernel, sizes), out_shape=(vmem((1,...  60.7 us
    pallas_call x1, Pallas kernels, write_outputs(): pl.pallas_call(functools.partial(write_kernel, count), out_shape=tuple((j...  2.29 us

profile of v7, /device:TPU:0, one launch (start us, length us, event | category | flops | bytes accessed | tf_op | source)
XLA Modules:
  0.0 63.7 jit_solution(10002468138370236340)
XLA Ops:
  0.6 60.7 %shard_map.171 = (f32[1,4]{1,0:T(1,128)S(1)}, f32[1,1]{1,0:T(1,128)}, bf16[512,1024]{1,0:T(8,128)(2,1)S(1)}, f32[32,1024]{1,0:T(8,128)S(1)}, f32[32,512]{1,0:T(8...) custom-call(bf16[512,1024]{1,0:T(8,128)(2,1)} %bitcast.8, s32[1,4]{1,0:T(1,128)} %lengths.1, f32[1,4]{1,0:T(1,128)} %teacher.1, ...), custom_call_target="tpu_custom_call" | custom-call | tf_op jit(solution)/shard_map/pallas_call | solution.py:1098
  61.4 2.3 %shard_map.172 = (f32[1,4]{1,0:T(1,128)}, f32[1,1]{1,0:T(1,128)}, bf16[512,1024]{1,0:T(8,128)(2,1)}, f32[32,1024]{1,0:T(8,128)}, f32[32,512]{1,0:T(8,128)}, /*index=5*/f32[32,512]{1,0:T(8,128)}, f32[32,1024]{1,0:T(8,128)}) custom-call(f32[1,4]{1,0:T(1,128)S(1)} %get-tuple-element.21.refs_0_, f32[1,1]{1,0:T(1,128)} %get-tuple-element.22.refs_1_, ...), custom_call_target="tpu_custom_call" | custom-call | tf_op jit(solution)/shard_map/pallas_call | solution.py:1073

commit v8 on v7

--- a/solution.py
+++ b/solution.py
@@ -997,11 +997,11 @@
 
     add_line(2)
     gather_context.tail()
+    for pair in range(3, pairs):
+        hidden_back(pair, 0)
+    gather_late.tail()
     for step in range(3, at.line_count + 1):
         own_sum = add_line(step)
-    gather_late.tail()
-    for pair in range(3, pairs):
-        hidden_back(pair, 0)
 
     gather_context.finish()
     gather_late.finish()

time: 63.8 us -> 64.7 us (1.014)
  Pallas kernels: 63 us -> 63.9 us
    pallas_call x1, Pallas kernels: 60.7 us -> 61.6 us  [run_step(): pl.pallas_call(functools.partial(step_kernel, sizes), out_shape=(vmem((1,...]
where the time goes in v8:
time: 64.7 us; the launch traced here: 64.5 us
  Pallas kernels  63.9 us (99%)
    pallas_call x1, Pallas kernels, run_step(): pl.pallas_call(functools.partial(step_kernel, sizes), out_shape=(vmem((1,...  61.6 us
    pallas_call x1, Pallas kernels, write_outputs(): pl.pallas_call(functools.partial(write_kernel, count), out_shape=tuple((j...  2.29 us

profile of v8, /device:TPU:0, one launch (start us, length us, event | category | flops | bytes accessed | tf_op | source)
XLA Modules:
  0.0 64.5 jit_solution(9912069115230419563)
XLA Ops:
  0.6 61.6 %shard_map.171 = (f32[1,4]{1,0:T(1,128)S(1)}, f32[1,1]{1,0:T(1,128)}, bf16[512,1024]{1,0:T(8,128)(2,1)S(1)}, f32[32,1024]{1,0:T(8,128)S(1)}, f32[32,512]{1,0:T(8...) custom-call(bf16[512,1024]{1,0:T(8,128)(2,1)} %bitcast.8, s32[1,4]{1,0:T(1,128)} %lengths.1, f32[1,4]{1,0:T(1,128)} %teacher.1, ...), custom_call_target="tpu_custom_call" | custom-call | tf_op jit(solution)/shard_map/pallas_call | solution.py:1098
  62.2 2.3 %shard_map.172 = (f32[1,4]{1,0:T(1,128)}, f32[1,1]{1,0:T(1,128)}, bf16[512,1024]{1,0:T(8,128)(2,1)}, f32[32,1024]{1,0:T(8,128)}, f32[32,512]{1,0:T(8,128)}, /*index=5*/f32[32,512]{1,0:T(8,128)}, f32[32,1024]{1,0:T(8,128)}) custom-call(f32[1,4]{1,0:T(1,128)S(1)} %get-tuple-element.21.refs_0_, f32[1,1]{1,0:T(1,128)} %get-tuple-element.22.refs_1_, ...), custom_call_target="tpu_custom_call" | custom-call | tf_op jit(solution)/shard_map/pallas_call | solution.py:1073
